TPU v7x, 256 devices: a whole 4x4x8 slice. The times are simulated.
256 devices in a mesh: leaf: 64 (over y, z, core), grid: 4 (over x).
Axes of the slice: x: 4, y: 4, z: 8, core: 2. Of those that a mesh axis runs over, the one named last changes fastest.
Arguments:
- source_leaf: float32 [8, 32768], P(None, ('leaf', 'grid')), may hold values from -6 to 6
- block_leaf: float32 [32768, 128], P(('leaf', 'grid')), may hold values from -0.5 to 0.5
- expand_leaf: float32 [32768, 128], P(('leaf', 'grid')), may hold values from -0.5 to 0.5
- basis_leaf: float32 [32768, 256], P(('leaf', 'grid')), may hold values from -0.25 to 0.25
- pivot_leaf: float32 [32768], P(('leaf', 'grid')), may hold values from -2 to 2
- couple_leaf: float32 [65536, 128], P(('leaf', 'grid')), may hold values from -0.5 to 0.5
- ranks_leaf: int32 [64, 2], replicated, may hold values from 32 to 128
- targets_leaf: int32 [65536], P(('leaf', 'grid')), may hold values from 0 to 16383, as said below
- source_middle: float32 [8, 32768], P(None, ('leaf', 'grid')), may hold values from -6 to 6
- block_middle: float32 [32768, 128], P(('leaf', 'grid')), may hold values from -0.5 to 0.5
- expand_middle: float32 [32768, 128], P(('leaf', 'grid')), may hold values from -0.5 to 0.5
- basis_middle: float32 [32768, 256], P(('leaf', 'grid')), may hold values from -0.0625 to 0.0625
- pivot_middle: float32 [32768], P(('leaf', 'grid')), may hold values from -2 to 2
- couple_middle: float32 [32768, 128], P(('leaf', 'grid')), may hold values from -0.5 to 0.5
- ranks_middle: int32 [4, 2], replicated, may hold values from 32 to 128
- targets_middle: int32 [32768], P(('leaf', 'grid')), may hold values from 0 to 32767, as said below
- source_upper: float32 [8, 32768], P(None, ('leaf', 'grid')), may hold values from -6 to 6
- block_upper: float32 [32768, 128], P(('leaf', 'grid')), may hold values from -0.5 to 0.5
- expand_upper: float32 [32768, 128], P(('leaf', 'grid')), may hold values from -0.5 to 0.5
- basis_upper: float32 [32768, 256], P(('leaf', 'grid')), may hold values from -0.046875 to 0.046875
- pivot_upper: float32 [32768], P(('leaf', 'grid')), may hold values from -2 to 2
- couple_upper: float32 [32768, 128], P(('leaf', 'grid')), may hold values from -0.5 to 0.5
- ranks_upper: int32 [2, 2], replicated, may hold values from 32 to 128
- targets_upper: int32 [32768], P(('leaf', 'grid')), may hold values from 0 to 32767, as said below
- source_root: float32 [8, 32768], P(None, ('leaf', 'grid')), may hold values from -6 to 6
- block_root: float32 [32768, 128], P(('leaf', 'grid')), may hold values from -0.5 to 0.5
- expand_root: float32 [32768, 128], P(('leaf', 'grid')), may hold values from -0.5 to 0.5
- basis_root: float32 [32768, 256], P(('leaf', 'grid')), may hold values from -0.03125 to 0.03125
- pivot_root: float32 [32768], P(('leaf', 'grid')), may hold values from -2 to 2
- ranks_root: int32 [1, 2], replicated, may hold values from 32 to 128
Outputs:
- answer_leaf: float32 [8, 32768], P(None, ('leaf', 'grid'))
- answer_middle: float32 [8, 32768], P(None, ('leaf', 'grid'))
- answer_upper: float32 [8, 32768], P(None, ('leaf', 'grid'))
- answer_root: float32 [8, 32768], P(None, ('leaf', 'grid'))
Inputs may be any that keep to these rules, and one draw needn't show every extreme that they name: `targets_leaf`: within one leaf front the 1024 entries are distinct; each names a row of the parent front's row vector of 16384 rows. Split that vector's separator part and its update part each evenly, in order, over the parent's devices (leaf then grid); then the rows of one device name at most 4 rows held by any one of them, and exactly that many for some. `targets_middle`: within one middle front the entries are distinct; each names a row of the parent front's row vector of 32768 rows. Split likewise over the parent's devices, the rows of one device name at most 1 row held by any one of them, and exactly that many for some. `targets_upper`: within one upper front the entries are distinct; each names a row of the root separator. Split evenly in order over all devices, the rows of one device name at most 1 row held by any one of them, and exactly that many for some.
All inputs are finite; a program needn't handle non-finite values.
Results may differ from a plain program's by a relative error of at most 0.0003.
Values sent between devices are 32-bit elements; how exact they have to be, the bound alone decides.
A program may use at most 128 MiB of HBM per device.

v0:
```python
import functools

import jax
import jax.numpy as jnp
from jax import lax
from jax.experimental import pallas as pl
from jax.experimental.pallas import tpu as pltpu
from jax.sharding import PartitionSpec as P

RANK = 128
LANES = 128
MESH = pl.DeviceIdType.MESH
F32 = jnp.float32
BF16 = jnp.bfloat16


def once(a, b, ca, cb):
    return lax.dot_general(a, b, (((ca,), (cb,)), ((), ())), preferred_element_type=F32)


def halves(x):
    hi = x.astype(BF16)
    return hi, (x - hi.astype(F32)).astype(BF16)


def dot(a, b, ca, cb):
    ah, al = halves(a)
    bh, bl = halves(b)
    if ca == 0:
        return once(ah, bh, ca, cb) + (once(al, bh, ca, cb) + once(ah, bl, ca, cb))
    n = a.shape[0]
    both = once(jnp.concatenate([ah.astype(F32), al.astype(F32)], axis=0).astype(BF16), bh, ca, cb)
    return both[:n] + (both[n:] + once(ah, bl, ca, cb))


def pieces3(x):
    hi = x.astype(BF16)
    rest = x - hi.astype(F32)
    mid = rest.astype(BF16)
    return hi, mid, (rest - mid.astype(F32)).astype(BF16)


def mult(a, b):
    return dot(a, b, 1, 0)


def outer(a, b):
    return dot(a, b, 1, 1)


def inner(a, b):
    return dot(a, b, 0, 0)


def split3(x):
    hi = x.astype(BF16).astype(F32)
    rest = x - hi
    mid = rest.astype(BF16).astype(F32)
    return jnp.concatenate([hi, mid, rest - mid], axis=0).astype(BF16)


def select(x, onehot, cb):
    out = once(split3(x), onehot, 1, cb)
    n = x.shape[0]
    return out[:n] + out[n : 2 * n] + out[2 * n :]


def kernel(cfg, names, *refs):
    leaves, across, size, ups, count, caps = cfg
    total_devices = leaves * across
    (src, blk, exp, bas, piv, rnk) = [refs[4 * i : 4 * i + 4] for i in range(6)]
    cpl = refs[24:27]
    tgt = refs[27:30]
    outs = refs[30:34]
    m = dict(zip(names, refs[34:-2]))
    send_sem, recv_sem = refs[-2:]
    sems = {}

    me = lax.axis_index("leaf") * across + lax.axis_index("grid")
    plane = size[1]
    planes = total_devices // plane
    spot = me % plane
    layer = me // plane
    late = total_devices > 64
    pending = []

    def where(peer):
        return (peer // across, peer % across)

    def sem_of(name):
        return sems.setdefault(name, len(sems))

    def remote(a, b, sem, peer):
        return pltpu.make_async_remote_copy(
            src_ref=a,
            dst_ref=b,
            send_sem=send_sem.at[sem],
            recv_sem=recv_sem.at[sem],
            device_id=where(peer),
            device_id_type=MESH,
        )

    def wait_for(part, sem):
        pltpu.make_async_copy(part, part, sem).wait()

    def send_each(source, dest, group, name, stride=1):
        idx = me // stride % group
        base = me - idx * stride
        sem = sem_of(name)

        def body(k, carry):
            q = (idx + k) % group
            remote(source(q), dest(idx), sem, base + q * stride).start()
            return carry

        lax.fori_loop(1, group, body, 0)

    def send_all(name, group, stride=1):
        buf = m[name]
        idx = me // stride % group
        send_each(lambda q: buf.at[idx], lambda i: buf.at[i], group, name, stride)
        pending.append((buf.at[pl.ds(0, group - 1)], sem_of(name)))

    def arrive(name, group):
        wait_for(m[name].at[pl.ds(0, group - 1)], recv_sem.at[sem_of(name)])

    barrier = pltpu.get_barrier_semaphore()

    def greet(k, carry):
        pl.semaphore_signal(
            barrier, inc=1, device_id=where((me + k) % total_devices), device_id_type=MESH
        )
        return carry

    lax.fori_loop(1, total_devices, greet, 0)

    col = lax.broadcasted_iota(jnp.int32, (count, RANK), 1)

    def mask(level, front, which):
        return (col < rnk[level][front, which]).astype(F32)

    def local_forward(level, b):
        local = mult(b, blk[level][...])
        bq = mult(b, bas[level][:, :RANK])
        lv = mult(local, bas[level][:, RANK:]) if level < 3 else None
        return local, bq, lv

    parts_of = [min(size[level], 16) for level in range(3)]

    def scatter_cross(level):
        g = size[level]
        p = parts_of[level]
        rp = RANK // p
        idx = me % g
        base = me - idx
        sem = sem_of(("rs", level))
        cross_p, rs_buf = m["cross_p", level], m["rs", level]

        def body(k, carry):
            q = (idx + k) % p

            def go():
                rows = pl.ds(pl.multiple_of(q * rp, 8), rp)
                remote(cross_p.at[rows], rs_buf.at[idx], sem, base + q).start()

            if g == p:
                go()
            else:
                pl.when(q != idx)(go)
            return carry

        lax.fori_loop(1 if g == p else 0, p, body, 0)

        def keep():
            rows = pl.ds(pl.multiple_of(idx * rp, 8), rp)
            rs_buf[idx] = cross_p[rows, :]

        if g == p:
            keep()
        else:
            pl.when(idx < p)(keep)

    def pack_couple(level):
        gp = size[level + 1]
        u = ups[level]
        cap = caps[level]
        wide = max(8, cap)
        sep = gp * LANES
        t = tgt[level][...]
        upd = t >= sep
        rel = jnp.where(upd, t - sep, t)
        dst = rel // LANES
        low = rel % LANES + jnp.where(upd, LANES, 0)
        ri = lax.broadcasted_iota(jnp.int32, (u, u), 0)
        ci = lax.broadcasted_iota(jnp.int32, (u, u), 1)
        dst_f = dst.astype(F32)
        dst_c = jnp.sum(jnp.where(ri == ci, jnp.broadcast_to(dst_f, (u, u)), 0.0), axis=1, keepdims=True)
        rank = jnp.sum(
            jnp.where((dst_c == dst_f) & (ri < ci), 1.0, 0.0), axis=0, keepdims=True
        ).astype(jnp.int32)
        pos = dst * wide + rank
        slots = gp * wide
        si = lax.broadcasted_iota(jnp.int32, (slots, u), 0)
        hit = (si == pos).astype(F32)
        hit16 = hit.astype(BF16)
        hi, mid, lo = [once(hit16, piece, 1, 0) for piece in pieces3(cpl[level][...])]
        moved = hi + mid + lo
        perm_buf, recv_c = m["perm", level], m["couple", level]
        if cap <= 4:
            shifted = (si == pos + 4).astype(F32)
            lowc = jnp.sum(shifted * low.astype(F32), axis=1, keepdims=True)
            both = moved + jnp.broadcast_to(lowc, (slots, LANES))
        else:
            lowc = jnp.sum(hit * low.astype(F32), axis=1, keepdims=True)
            both = jnp.concatenate([moved, jnp.broadcast_to(lowc, (slots, LANES))], axis=1)
        perm_buf[...] = both.reshape(gp, wide, both.shape[1])
        idx = me % gp
        recv_c[idx] = perm_buf[idx]

    def ship_couple(level):
        gp = size[level + 1]
        perm_buf, recv_c = m["perm", level], m["couple", level]
        send_each(lambda q: perm_buf.at[q], lambda i: recv_c.at[i], gp, ("couple", level))
        pending.append((perm_buf.at[pl.ds(0, gp - 1)], sem_of(("couple", level))))

    def gather_cross(level):
        g = size[level]
        gp = size[level + 1]
        p = parts_of[level]
        idx = me % g
        place = me % gp
        sem = sem_of(("cross", level))
        slot = place // g * p + idx
        buf, rs_buf = m["cross", level], m["rs", level]

        def go():
            wait_for(rs_buf.at[pl.ds(0, g - 1)], recv_sem.at[sem_of(("rs", level))])
            buf[slot] = jnp.sum(rs_buf[...], axis=0)

            def body(k, carry):
                peer = me - place + (place + k) % gp
                remote(buf.at[slot], buf.at[slot], sem, peer).start()
                return carry

            lax.fori_loop(1, gp, body, 0)

        if g == p:
            go()
        else:
            pl.when(idx < p)(go)

    def build_gt(level):
        g = size[level]
        gp = size[level + 1]
        wide = max(8, caps[level])
        nch = gp // g
        gt = m["gt", level]
        rows = gt.shape[1]
        arrive(("couple", level), gp)
        slots = g * wide
        lane = lax.broadcasted_iota(jnp.int32, (slots, rows), 1).astype(F32)
        for child in range(nch):
            got = m["couple", level][child * g : (child + 1) * g]
            got = got.reshape(slots, got.shape[2])
            if caps[level] <= 4:
                up = jnp.concatenate([got[4:, :1], got[:4, :1]], axis=0)
                si = lax.broadcasted_iota(jnp.int32, (slots, 1), 0)
                low = jnp.where(si % 8 < 4, up, -1.0)
            else:
                low = got[:, LANES : LANES + 1]
            ot = (lane == low).astype(F32).astype(BF16)
            hi, mid, lo = [once(piece, ot, 0, 0) for piece in pieces3(got[:, :LANES])]
            gt[child * RANK : (child + 1) * RANK, :] = hi + mid + lo

    def arrive_cross(level):
        g = size[level]
        p = parts_of[level]
        n = size[level + 1] // g * p
        sem = recv_sem.at[sem_of(("cross", level))]
        buf = m["cross", level]
        if g == p:
            wait_for(buf.at[pl.ds(0, n - 1)], sem)
        else:
            idx = me % g
            pl.when(idx < p)(lambda: wait_for(buf.at[pl.ds(0, n - 1)], sem))
            pl.when(idx >= p)(lambda: wait_for(buf.at[pl.ds(0, n)], sem))

    def cross_of(level, child):
        p = parts_of[level]
        return m["cross", level][pl.ds(child * p, p)].reshape(RANK, RANK)

    def build_bot_middle():
        gp = size[2]
        place = me % gp
        rows = 2 * LANES
        ri = lax.broadcasted_iota(jnp.int32, (rows, LANES), 0)
        arrive("tgt_middle", gp)
        mine = jnp.where(ri < LANES, place * LANES + ri, (gp + place - 1) * LANES + ri).astype(F32)

        def fill(j, carry):
            t = m["tgt_middle"][j][0:1, :]
            lanes = pl.ds(pl.multiple_of(j * LANES, LANES), LANES)
            m["bot_middle"][:, lanes] = (mine == t).astype(F32).astype(BF16)
            return carry

        lax.fori_loop(0, gp, fill, 0)

    def build_bot_upper():
        rows = planes * LANES
        ri = lax.broadcasted_iota(jnp.int32, (rows, LANES), 0)
        arrive("tgt_upper", plane)
        mine = ((ri // LANES * plane + spot) * LANES + ri % LANES).astype(F32)

        def fill(j, carry):
            t = m["tgt_upper"][j][0:1, :]
            lanes = pl.ds(pl.multiple_of(j * LANES, LANES), LANES)
            m["bot_upper"][:, lanes] = (mine == t).astype(F32).astype(BF16)
            return carry

        lax.fori_loop(0, plane, fill, 0)

    def build_ft_middle():
        t = tgt[1][...]
        ri = lax.broadcasted_iota(jnp.int32, (LANES, LANES), 0)

        def fill(j, carry):
            rows = pl.ds(pl.multiple_of(j * LANES, LANES), LANES)
            m["ft_middle"][rows, :] = (ri + j * LANES == t).astype(F32).astype(BF16)
            return carry

        lax.fori_loop(0, m["ft_middle"].shape[0] // LANES, fill, 0)

    def build_ft_upper():
        arrive("tgt_layer", planes)
        t = jnp.concatenate([m["tgt_layer"][j][0:1, :] for j in range(planes)], axis=1)
        ri = lax.broadcasted_iota(jnp.int32, (LANES, planes * LANES), 0)

        def fill(j, carry):
            rows = pl.ds(pl.multiple_of(j * LANES, LANES), LANES)
            here = ((ri + (layer * plane + j) * LANES).astype(F32) == t).astype(F32)
            m["ft_upper"][rows, :] = here.astype(BF16)
            return carry

        lax.fori_loop(0, plane, fill, 0)

    def total_sum(value, name):
        m[name, "a"][spot] = value
        send_all((name, "a"), plane)
        arrive((name, "a"), plane)
        m[name, "b"][layer] = jnp.sum(m[name, "a"][...], axis=0)
        send_all((name, "b"), planes, plane)

    def total_arrived(name):
        arrive((name, "b"), planes)
        return jnp.sum(m[name, "b"][...], axis=0)

    def share(level, zp):
        m["zp", level][me % size[level]] = zp
        send_all(("zp", level), size[level])

    def shared(level):
        arrive(("zp", level), size[level])
        return jnp.sum(m["zp", level][...], axis=0)

    local, bq, lv = local_forward(0, src[0][...])
    m["f1"][spot] = jnp.concatenate([bq, lv], axis=0)
    for level in range(3):
        m["cross_p", level][...] = inner(exp[level][...], bas[level][:, RANK:])
        pack_couple(level)
    pl.semaphore_wait(barrier, total_devices - 1)
    send_all("f1", plane)
    scatter_cross(0)
    ship_couple(0)
    for level in (1, 2):
        scatter_cross(level)
    m["tgt_middle"][me % size[2]] = jnp.broadcast_to(tgt[1][...], (8, LANES)).astype(F32)
    send_all("tgt_middle", size[2])
    gather_cross(0)
    ship_couple(1)
    gather_cross(1)
    mine_t = jnp.broadcast_to(tgt[2][...], (8, LANES)).astype(F32)
    m["tgt_upper"][spot] = mine_t
    send_all("tgt_upper", plane)
    m["tgt_layer"][layer] = mine_t
    send_all("tgt_layer", planes, plane)
    build_gt(0)

    saved = []
    inc_upd = None
    for level in range(3):
        g = size[level]
        gp = size[level + 1]
        nch = gp // g
        place = me % gp
        parent = me // gp
        child_me = place // g
        arrive_cross(level)
        if level < 2:
            name = ("f1", "f2")[level]
            buf, step = m[name], g
            arrive(name, gp)
        else:
            buf, step = m["f3b"], g // plane
            arrive("f3b", planes)
        ws = []
        for child in range(nch):
            tot = jnp.sum(buf[child * step : (child + 1) * step, : 2 * count, :], axis=0)
            front = parent * nch + child
            hq = tot[:count] * mask(level, front, 0)
            cross = cross_of(level, child)
            ws.append((tot[count:] + mult(hq, cross)) * mask(level, front, 1))
        inc = -mult(jnp.concatenate(ws, axis=1), m["gt", level][...])
        if level == 1:
            rows = jnp.concatenate([buf[j, 2 * count : 3 * count, :] for j in range(gp)], axis=1)
            inc = inc + select(rows, m["bot_middle"][...], 1)
        if level == 2:
            inc = inc + jnp.sum(buf[:, 2 * count : 3 * count, :], axis=0)
        bn = src[level + 1][...] + inc[:, :LANES]
        local_n, bq_n, lv_n = local_forward(level + 1, bn)
        if level == 0:
            m["f2"][me % size[2]] = jnp.concatenate([bq_n, lv_n, inc[:, LANES:]], axis=0)
            send_all("f2", size[2])
        elif level == 1:
            m["f3a"][spot] = jnp.concatenate([bq_n, lv_n, inc[:, LANES:]], axis=0)
            send_all("f3a", plane)
        else:
            m["f4", "a"][spot] = bq_n
            send_all(("f4", "a"), plane)
        own = jnp.sum(buf[pl.ds(child_me * step, step), :count, :], axis=0)
        hq = own * mask(level, me // g, 0)
        z = (local + outer(hq, exp[level][...])) * piv[level][...]
        saved.append(z)
        share(level, mult(z, exp[level][...]))
        if level == 0:
            ship_couple(2)
            gather_cross(2)
            build_gt(1)
            build_bot_middle()
        elif level == 1:
            build_bot_upper()
            arrive("f3a", plane)
            sums = jnp.sum(m["f3a"][:, : 2 * count, :], axis=0)
            rows = jnp.concatenate([m["f3a"][j, 2 * count :, :] for j in range(plane)], axis=1)
            part = select(rows, m["bot_upper"][...], 1)
            for q in range(planes):
                m["f3s"][q] = jnp.concatenate([sums, part[:, q * LANES : (q + 1) * LANES]], axis=0)
            m["f3b"][layer] = m["f3s"][layer]
            send_each(lambda q: m["f3s"].at[q], lambda i: m["f3b"].at[i], planes, "f3b", plane)
            pending.append((m["f3s"].at[pl.ds(0, planes - 1)], sem_of("f3b")))
            build_gt(2)
        else:
            arrive(("f4", "a"), plane)
            m["f4", "b"][layer] = jnp.sum(m["f4", "a"][...], axis=0)
            send_all(("f4", "b"), planes, plane)
        local = local_n

    build_ft_upper()
    hq = total_arrived("f4") * mask(3, 0, 0)
    z = (local + outer(hq, exp[3][...])) * piv[3][...]
    total_sum(mult(z, exp[3][...]), "f5")
    if not late:
        build_ft_middle()
    x = outer(z, blk[3][...])
    rp_total = total_arrived("f5") * mask(3, 0, 0)
    x = x + outer(rp_total, bas[3][:, :RANK])

    xu = None
    for level in (2, 1, 0):
        g = size[level]
        gp = size[level + 1]
        nch = gp // g
        place = me % gp
        child_me = place // g
        full = x if xu is None else jnp.concatenate([x, xu], axis=1)
        sp = outer(full, m["gt", level][...])
        pieces = [sp[:, c * RANK : (c + 1) * RANK] for c in range(nch)]
        if level == 2:
            m["b1a"][spot] = jnp.concatenate(pieces + [x], axis=0)
            send_all("b1a", plane)
            outs[3][...] = x
            arrive("b1a", plane)
            o = nch * count
            sums = jnp.sum(m["b1a"][:, :o, :], axis=0)
            rows = jnp.concatenate([m["b1a"][j, o:, :] for j in range(plane)], axis=1)
            part = select(rows, m["ft_upper"][...], 0)
            for q in range(planes):
                c = q * plane // g
                m["b1s"][q] = jnp.concatenate(
                    [sums[c * count : (c + 1) * count], part[:, q * LANES : (q + 1) * LANES]], axis=0
                )
            m["b1b"][layer] = m["b1s"][layer]
            send_each(lambda q: m["b1s"].at[q], lambda i: m["b1b"].at[i], planes, "b1b", plane)
            pending.append((m["b1s"].at[pl.ds(0, planes - 1)], sem_of("b1b")))
            arrive("b1b", planes)
            both = jnp.sum(m["b1b"][...], axis=0)
            s, xu = both[:count], both[count:]
        else:
            name = ("b3", "b2")[level]
            buf, piece = m[name], m["piece", level]
            for c in range(nch):
                piece[c] = pieces[c]
            head = pl.ds(0, count)
            rest = pl.ds(count, 2 * count)
            buf[place, head] = piece[child_me]
            if level == 1:
                buf[place, rest] = jnp.concatenate([x, xu], axis=0)

                def ship(k, carry, gp=gp, g=g, place=place, buf=buf, piece=piece, name=name):
                    q = (place + k) % gp
                    peer = me - place + q
                    sem = sem_of(name)
                    remote(piece.at[q // g], buf.at[place, head], sem, peer).start()
                    remote(buf.at[place, rest], buf.at[place, rest], sem, peer).start()
                    return carry

                lax.fori_loop(1, gp, ship, 0)
            else:
                send_each(lambda q: piece.at[q // g], lambda i: buf.at[i], gp, name)
            pending.append((buf.at[pl.ds(0, gp - 1)], sem_of(name)))
            outs[level + 1][...] = x
            arrive(name, gp)
            s = jnp.sum(buf[:, head, :], axis=0)
            if level == 1:
                blocks = [buf[j, count : 2 * count, :] for j in range(gp)]
                blocks += [buf[j, 2 * count :, :] for j in range(gp)]
                if late:
                    build_ft_middle()
                xu = select(jnp.concatenate(blocks, axis=1), m["ft_middle"][...], 0)
        s = s * mask(level, me // g, 1)
        r = saved[level] - outer(s, bas[level][:, RANK:])
        proj = (shared(level) - outer(s, cross_of(level, child_me))) * mask(level, me // g, 0)
        x = outer(r, blk[level][...]) + outer(proj, bas[level][:, :RANK])
    outs[0][...] = x

    for part, sem in pending:
        wait_for(part, send_sem.at[sem])
    for level in range(3):
        g = size[level]
        p = parts_of[level]
        rp = RANK // p
        n = size[level + 1] // g * p
        idx = me % g
        rs_sem = send_sem.at[sem_of(("rs", level))]
        ag_sem = send_sem.at[sem_of(("cross", level))]
        cross_p, buf = m["cross_p", level], m["cross", level]

        def ag_done():
            for _ in range(g // p - 1):
                wait_for(buf.at[pl.ds(0, n)], ag_sem)
            wait_for(buf.at[pl.ds(0, n - 1)], ag_sem)

        if g == p:
            wait_for(cross_p.at[pl.ds(0, (p - 1) * rp)], rs_sem)
            ag_done()
        else:
            pl.when(idx < p)(lambda: wait_for(cross_p.at[pl.ds(0, (p - 1) * rp)], rs_sem))
            pl.when(idx >= p)(lambda: wait_for(cross_p, rs_sem))
            pl.when(idx < p)(ag_done)


def solution(mesh):
    leaves, across = mesh.shape["leaf"], mesh.shape["grid"]

    def shards(*args):
        levels = [args[8 * i : 8 * i + 8] for i in range(3)]
        root = args[24:30]
        (sl, bl, el, qs, pv, cl, rk, tg) = zip(*levels)
        src = list(sl) + [root[0]]
        blk = list(bl) + [root[1]]
        exp = list(el) + [root[2]]
        bas = list(qs) + [root[3]]
        piv = [v.reshape(1, -1) for v in list(pv) + [root[4]]]
        rnk = list(rk) + [root[5]]
        tgt = [t.reshape(1, -1) for t in tg]
        count = src[0].shape[0]
        ups = [t.shape[1] for t in tgt]
        fronts = [r.shape[0] for r in rnk]
        size = [leaves * across // f for f in fronts]
        for v in src:
            assert v.shape[1] == LANES
        vm = lambda *s: pltpu.VMEM(s, F32)
        bits = lambda *s: pltpu.VMEM(s, BF16)
        total = leaves * across
        plane = size[1]
        planes = total // plane
        nch = [size[i + 1] // size[i] for i in range(3)]
        caps = [max(1, -(-ups[i] // size[i + 1])) for i in range(3)]
        parts = [min(size[i], 16) for i in range(3)]
        ft = (size[2] * 2 * LANES, LANES)
        bufs = {
            "f1": vm(plane, 2 * count, LANES),
            "f2": vm(size[2], 3 * count, LANES),
            "f3a": vm(plane, 3 * count, LANES),
            "f3s": vm(planes, 3 * count, LANES),
            "f3b": vm(planes, 3 * count, LANES),
            "b1a": vm(plane, (nch[2] + 1) * count, LANES),
            "b1s": vm(planes, 2 * count, LANES),
            "b1b": vm(planes, 2 * count, LANES),
            "b2": vm(size[2], 3 * count, LANES),
            "b3": vm(size[1], count, LANES),
            "tgt_middle": vm(size[2], 8, LANES),
            "tgt_upper": vm(plane, 8, LANES),
            "tgt_layer": vm(planes, 8, LANES),
            "bot_middle": bits(2 * LANES, size[2] * LANES),
            "bot_upper": bits(planes * LANES, plane * LANES),
            "ft_middle": bits(*ft),
            "ft_upper": bits(plane * LANES, planes * LANES),
        }
        for name in ("f4", "f5"):
            bufs[name, "a"] = vm(plane, count, LANES)
            bufs[name, "b"] = vm(planes, count, LANES)
        for i in range(3):
            wide = LANES if caps[i] <= 4 else 2 * LANES
            bufs["perm", i] = vm(size[i + 1], max(8, caps[i]), wide)
            bufs["couple", i] = vm(size[i + 1], max(8, caps[i]), wide)
            bufs["cross_p", i] = vm(RANK, RANK)
            bufs["rs", i] = vm(size[i], RANK // parts[i], RANK)
            bufs["cross", i] = vm(nch[i] * parts[i], RANK // parts[i], RANK)
            bufs["gt", i] = vm(nch[i] * RANK, LANES * (1 if i == 2 else 2))
            bufs["zp", i] = vm(size[i], count, LANES)
            bufs["piece", i] = vm(nch[i], count, LANES)
        scratch = list(bufs.values())
        scratch += [pltpu.SemaphoreType.DMA((40,)), pltpu.SemaphoreType.DMA((40,))]
        vspec = pl.BlockSpec(memory_space=pltpu.VMEM)
        sspec = pl.BlockSpec(memory_space=pltpu.SMEM)
        return pl.pallas_call(
            functools.partial(kernel, (leaves, across, size, ups, count, caps), list(bufs)),
            out_shape=[jax.ShapeDtypeStruct(v.shape, F32) for v in src],
            in_specs=[vspec] * 20 + [sspec] * 4 + [vspec] * 6,
            out_specs=[vspec] * 4,
            scratch_shapes=scratch,
            compiler_params=pltpu.CompilerParams(
                collective_id=0, has_side_effects=True, vmem_limit_bytes=60 * 1024 * 1024
            ),
        )(*src, *blk, *exp, *bas, *piv, *rnk, *cl, *tgt)

    spread = ("leaf", "grid")
    level = (P(None, spread), P(spread, None), P(spread, None), P(spread, None), P(spread))
    mid = level + (P(spread, None), P(), P(spread))
    return jax.shard_map(
        shards,
        mesh=mesh,
        in_specs=mid * 3 + level + (P(),),
        out_specs=(P(None, spread),) * 4,
        check_vma=False,
    )
```

profile of v0, /device:TPU:1, one launch (start us, length us, event | category | flops | bytes accessed | tf_op | source)
XLA Modules:
  0.0 316.1 jit_solution(6336283333187925512)
XLA Ops:
  0.6 0.0 copy-start.4
  0.6 0.7 copy-done.4
  1.3 0.0 copy-start.5
  1.3 0.7 copy.35.refs_21_
  2.0 0.0 copy-done.5
  2.0 0.7 copy.34.refs_20_
  2.7 310.1 %shard_map.309 = (f32[8,128]{1,0:T(8,128)}, f32[8,128]{1,0:T(8,128)}, f32[8,128]{1,0:T(8,128)}, f32[8,128]{1,0:T(8,128)}) custom-call(f32[8,128]{1,0:T(8,128)} %refs_0_.1, f32[8,128]{1,0:T(8,128)} %refs_1_.1, f32[8,128]{1,0:T(8,128)} %refs_2_.1, f32[8,128]{1,0:T(8,128)} %refs_3_.1, f32[128,128]{1,0:T(8,128)} %refs_4_.1, f32[128,128]{1,0:T(8,128)} %refs_5_.1, ...), custom_call_target="tpu_custom_call" | custom-call | tf_op jit(solution)/shard_map/pallas_call | solution.py:626
  312.8 0.0 copy-start.3
  312.8 0.7 copy-done.3
  313.5 0.0 copy-start.2
  313.5 0.6 copy.40
  314.1 0.1 copy-done.2
  314.2 0.0 copy-start.1
  314.2 0.6 copy.41
  314.8 0.1 copy-done.1
  314.9 0.0 copy-start
  314.9 0.6 copy.42
  315.5 0.1 copy-done
  315.6 0.6 copy.43
Async XLA Ops:
  0.6 0.7 copy-start.4
  1.3 0.7 copy-start.5
  312.8 0.7 copy-start.3
  313.5 0.7 copy-start.2
  314.2 0.7 copy-start.1
  314.9 0.7 copy-start
where the time goes:
time: 316 us
  Pallas kernels  310 us (98%)
  local copies, waits for them, and re-layouts  5.35 us (2%)
    pallas_call x1, Pallas kernels, shards(): pl.pallas_call(functools.partial(kernel, (leaves, across, size, ups, coun...  310 us

commit v1 on v0

v1 whole, which is shorter than its diff:
```python
import functools

import jax
import jax.numpy as jnp
from jax import lax
from jax.experimental import pallas as pl
from jax.experimental.pallas import tpu as pltpu
from jax.sharding import PartitionSpec as P

RANK = 128
LANES = 128
NEAR = 8
MESH = pl.DeviceIdType.MESH
F32 = jnp.float32
BF16 = jnp.bfloat16


def once(a, b, ca, cb):
    return lax.dot_general(a, b, (((ca,), (cb,)), ((), ())), preferred_element_type=F32)


def halves(x):
    hi = x.astype(BF16)
    return hi, (x - hi.astype(F32)).astype(BF16)


def stacked(x):
    hi = x.astype(BF16).astype(F32)
    return jnp.concatenate([hi, x - hi], axis=0).astype(BF16)


def times(a, b, cb):
    bh, bl = b
    n = a.shape[0]
    both = once(stacked(a), bh, 1, cb)
    return both[:n] + (both[n:] + once(a.astype(BF16), bl, 1, cb))


def mult(a, b):
    return times(a, halves(b), 0)


def outer(a, b):
    return times(a, halves(b), 1)


def inner(a, b):
    ah, al = halves(a)
    bh, bl = halves(b)
    return once(ah, bh, 0, 0) + (once(al, bh, 0, 0) + once(ah, bl, 0, 0))


def pick(x, onehot):
    n = x.shape[0]
    both = once(stacked(x), onehot, 1, 1)
    return both[:n] + both[n:]


def spread(rows, onehot, groups, count):
    m = groups * count
    wide = onehot.shape[1] // groups
    both = once(stacked(rows.T[:m]), onehot, 1, 0)
    out = None
    for g in range(groups):
        lanes = slice(g * wide, (g + 1) * wide)
        part = both[g * count : (g + 1) * count, lanes] + both[m + g * count : m + (g + 1) * count, lanes]
        out = part if out is None else out + part
    return out


def diagonal(x, groups):
    count, wide = x.shape
    zero = jnp.zeros((count, wide), F32)
    rows = [
        jnp.concatenate([x if h == g else zero for h in range(groups)], axis=1) for g in range(groups)
    ]
    rows.append(jnp.zeros((LANES - groups * count, groups * wide), F32))
    return jnp.concatenate(rows, axis=0)


def kernel(cfg, names, *refs):
    leaves, across, size, ups, count, cap = cfg
    total_devices = leaves * across
    (src, blk, exp, bas, piv, rnk) = [refs[4 * i : 4 * i + 4] for i in range(6)]
    cpl = refs[24:27]
    tgt = refs[27:30]
    outs = refs[30:34]
    m = dict(zip(names, refs[34:-3]))
    send_sem, recv_sem, ready = refs[-3:]
    sems = {}
    parts = {}

    me = lax.axis_index("leaf") * across + lax.axis_index("grid")
    near = me % NEAR
    far = me // NEAR
    nb = [s // NEAR for s in size]
    plane = size[1]
    fars = nb[3]

    def where(peer):
        return (peer // across, peer % across)

    def sem_of(name):
        return sems.setdefault(name, len(sems))

    def remote(a, b, sem, peer):
        return pltpu.make_async_remote_copy(
            src_ref=a,
            dst_ref=b,
            send_sem=send_sem.at[sem],
            recv_sem=recv_sem.at[sem],
            device_id=where(peer),
            device_id_type=MESH,
        )

    def wait_for(part, sem):
        pltpu.make_async_copy(part, part, sem).wait()

    def fan(group, stride, *sets):
        idx = me // stride % group
        base = me - idx * stride
        for name, source, dest, part in sets:
            sem_of(name)
            parts[name] = part

        def body(k, carry):
            q = (idx + k) % group
            for name, source, dest, part in sets:
                remote(source(q), dest(idx), sem_of(name), base + q * stride).start()
            return carry

        lax.fori_loop(1, group, body, 0)

    def arrive(name):
        wait_for(parts[name], recv_sem.at[sem_of(name)])

    def slots(name, group):
        buf = m[name]
        return buf.at[pl.ds(0, group - 1)]

    def spread_own(name, group, stride):
        buf = m[name]
        idx = me // stride % group
        fan(group, stride, (name, lambda q: buf.at[idx], lambda i: buf.at[i], slots(name, group)))

    barrier = pltpu.get_barrier_semaphore()

    def greet_near(sem):
        def body(k, carry):
            peer = far * NEAR + (near + k) % NEAR
            pl.semaphore_signal(sem, inc=1, device_id=where(peer), device_id_type=MESH)
            return carry

        lax.fori_loop(1, NEAR, body, 0)

    def greet_far(k, carry):
        peer = (far + k) % fars * NEAR + near
        pl.semaphore_signal(barrier, inc=1, device_id=where(peer), device_id_type=MESH)
        return carry

    lax.fori_loop(1, fars, greet_far, 0)
    greet_near(barrier)

    col = lax.broadcasted_iota(jnp.int32, (count, RANK), 1)

    def mask(level, which):
        def of(front):
            rank = rnk[level][which, front] if level < 3 else rnk[level][0, which]
            return (col < rank).astype(F32)

        return of

    front = [me // s for s in size]
    head = [mask(level, 0)(front[level]) for level in range(4)]
    side = [mask(level, 1)(front[level]) for level in range(3)]

    def q_of(level):
        return bas[level][:, :RANK]

    def v_of(level):
        return bas[level][:, RANK:]

    def tiles_of(level):
        n = nb[level + 1]
        return NEAR * n // LANES, LANES // n

    four = size[0]
    my4 = me % four
    s0 = src[0][...]
    local0 = mult(s0, blk[0][...])
    m["f1"][my4] = jnp.concatenate([mult(s0, q_of(0)), mult(local0, v_of(0))], axis=0)
    m["c0"][my4] = inner(exp[0][...], v_of(0))

    slice_rows = RANK // NEAR
    root_piv = jnp.broadcast_to(piv[3][...], (LANES, LANES)).T
    crosses = [
        inner(exp[1][...], v_of(1)),
        inner(exp[2][...], v_of(2)),
        inner(exp[3][...] * root_piv, exp[3][...]),
    ]
    for j, cross in enumerate(crosses):
        m["xp"][:, j * slice_rows : (j + 1) * slice_rows, :] = cross.reshape(NEAR, slice_rows, RANK)

    def split_targets(level):
        sep = size[level + 1] * LANES
        t = tgt[level][...]
        upd = t >= sep
        rel = jnp.where(upd, t - sep, t)
        return rel // LANES, rel % LANES + jnp.where(upd, LANES, 0)

    def pack_leaf():
        u = ups[0]
        dst, low = split_targets(0)
        ri = lax.broadcasted_iota(jnp.int32, (u, u), 0)
        ci = lax.broadcasted_iota(jnp.int32, (u, u), 1)
        dst_f = dst.astype(F32)
        dst_c = jnp.sum(jnp.where(ri == ci, jnp.broadcast_to(dst_f, (u, u)), 0.0), axis=1, keepdims=True)
        rank = jnp.sum(
            jnp.where((dst_c == dst_f) & (ri < ci), 1.0, 0.0), axis=0, keepdims=True
        ).astype(jnp.int32)
        slot = rank * plane + dst
        ch, cl = halves(cpl[0][...])
        lowmat = None
        li = lax.broadcasted_iota(jnp.int32, (LANES, u), 0)
        for s in range(cap):
            si = lax.broadcasted_iota(jnp.int32, (plane, u), 0) + s * plane
            hit = (si == slot).astype(F32).astype(BF16)
            lanes = slice(s * RANK, (s + 1) * RANK)
            m["hch"][:, lanes] = once(hit, ch, 1, 0).astype(BF16)
            m["hcl"][:, lanes] = once(hit, cl, 1, 0).astype(BF16)
            mine = jnp.where(li == cap * count + s, low.astype(F32), 0.0).astype(BF16)
            part = once(hit, mine, 1, 1)
            lowmat = part if lowmat is None else lowmat + part
        m["low0"][...] = lowmat

    def pack_couple(level):
        n = nb[level + 1]
        dst, low = split_targets(level)
        slot = dst % NEAR * n + dst // NEAR
        si = lax.broadcasted_iota(jnp.int32, (NEAR * n, LANES), 0)
        h = (si == slot).astype(F32).astype(BF16)
        m["h", level][...] = h
        hi, lo = [once(h, piece, 1, 0) for piece in halves(cpl[level][...])]
        m["pa", level][...] = (hi + lo).reshape(NEAR, n, RANK)
        rows = jnp.broadcast_to(low, (count, LANES)).astype(F32).astype(BF16)
        bi = lax.broadcasted_iota(jnp.int32, (n, LANES), 0) * NEAR
        m["ohr", level][...] = jnp.concatenate(
            [(bi + k == dst).astype(F32) for k in range(NEAR)], axis=1
        ).astype(BF16)
        return once(rows, h, 1, 1)

    low1, low2 = pack_couple(1), pack_couple(2)
    ri = lax.broadcasted_iota(jnp.int32, (count, LANES), 0)
    for t in range(2):
        two = low2[:, t * LANES : (t + 1) * LANES]
        m["lows"][t] = jnp.where(ri == 0, two, jnp.where(ri == 1, low1, 0.0))
    pack_leaf()

    pl.semaphore_wait(barrier, NEAR - 1 + fars - 1)
    greet_near(ready)
    spread_own("f1", four, 1)
    spread_own("c0", four, 1)

    def fan_near(name, source, dest):
        fan(NEAR, 1, (name, source, lambda i: dest.at[i], dest.at[pl.ds(0, NEAR - 1)]))

    m["xra"][near] = m["xp"][near]
    fan_near("xra", lambda q: m["xp"].at[q], m["xra"])
    m["la"][near] = m["lows"][near // 4]
    fan_near("la", lambda q: m["lows"].at[q // 4], m["la"])
    for level in (1, 2):
        pa, ra = m["pa", level], m["ra", level]
        ra[near] = pa[near]
        fan_near(("ra", level), lambda q, pa=pa: pa.at[q], ra)

    def keep(name, value):
        hi, lo = halves(value)
        m[name, "h"][...] = hi
        m[name, "l"][...] = lo

    def kept(name):
        return m[name, "h"][...], m[name, "l"][...]

    for level in (1, 2):
        wv = mult(blk[level][...], v_of(level))
        keep(("qw", level), jnp.concatenate([q_of(level), wv], axis=1))
    wpp = mult(blk[3][...] * piv[3][...], exp[3][...])
    keep(("qw", 3), jnp.concatenate([q_of(3), wpp], axis=1))

    arrive("f1")
    arrive("c0")
    cross0 = jnp.sum(m["c0"][...], axis=0)
    tot = jnp.sum(m["f1"][...], axis=0)
    hq0 = tot[:count] * head[0]
    keep(("cross", 0), cross0)
    w0 = (tot[count:] + times(hq0, kept(("cross", 0)), 0)) * side[0]

    def leaf_rows(a, b):
        ah, al = a
        bh, bl = halves(b)
        out = once(ah, bh, 1, 1) + once(ah, bl, 1, 1)
        return out if al is None else out + once(al, bh, 1, 1)

    place = me % plane

    def send_leaf(rows, got, name):
        m[got][pl.ds(place, 1), :] = m[rows][pl.ds(place, 1), :]
        fan(
            plane,
            1,
            (
                name,
                lambda q: m[rows].at[pl.ds(q, 1)],
                lambda i: m[got].at[pl.ds(i, 1)],
                m[got].at[pl.ds(0, plane - 1)],
            ),
        )

    hc = (m["hch"][...], m["hcl"][...])
    m["s0"][...] = leaf_rows(hc, diagonal(-w0, cap)) + m["low0"][...]
    pl.semaphore_wait(ready, NEAR - 1)
    send_leaf("s0", "r0", "r0")

    z0 = (local0 + outer(hq0, exp[0][...])) * piv[0][...]
    m["zx"][my4] = mult(z0, exp[0][...])
    spread_own("zx", four, 1)

    def store_row(buf, i, row):
        buf[pl.ds(i, 1), :] = row

    def forward_rows(level, table, got, name):
        n = nb[level + 1]
        per = tiles_of(level)[1]
        idx = far % n
        first = near % per * n
        store_row(m[got], idx, m[table][pl.ds(first + idx, 1), :])
        return (
            name,
            lambda q: m[table].at[pl.ds(first + q, 1)],
            lambda i: m[got].at[pl.ds(i, 1)],
            m[got].at[pl.ds(0, n - 1)],
        )

    def transposed(x):
        return jnp.concatenate([x, jnp.zeros((LANES - x.shape[0], LANES), F32)], axis=0).T

    def couple_set(level):
        n = nb[level + 1]
        ra, rb = m["ra", level], m["rb", level]
        idx = far % n
        rb[:, pl.ds(idx, 1), :] = ra[:, pl.ds(idx, 1), :]
        return (
            ("rb", level),
            lambda q: ra.at[:, pl.ds(q, 1)],
            lambda i: rb.at[:, pl.ds(i, 1)],
            rb.at[:, pl.ds(0, n - 1)],
        )

    arrive("xra")
    sums = jnp.sum(m["xra"][...], axis=0)
    for j, n in enumerate((nb[1], nb[2], nb[3])):
        m["xb", j][far % n] = sums[j * slice_rows : (j + 1) * slice_rows]
    spread_own(("xb", 0), nb[1], NEAR)
    arrive("la")
    m["tl"][...] = transposed(m["la"][...].reshape(NEAR * count, LANES))
    for level in (1, 2):
        arrive(("ra", level))
        fan(nb[level + 1], NEAR, forward_rows(level, "tl", ("lb", level), ("lb", level)), couple_set(level))
        spread_own(("xb", level), nb[level + 1], NEAR)

    def build(level):
        n = nb[level + 1]
        wide = 2 * LANES if level == 1 else LANES
        arrive(("lb", level))
        lb = m["lb", level][...]
        lane = lax.broadcasted_iota(jnp.int32, (n, wide), 1).astype(F32)
        at = 2 - level
        hits = [(lane == lb[:, k * count + at : k * count + at + 1]).astype(F32) for k in range(NEAR)]
        m["ohf", level][...] = jnp.concatenate(hits, axis=1).astype(BF16)
        m["ohg", level][...] = jnp.concatenate(hits, axis=0).astype(BF16)
        arrive(("rb", level))
        half = n // 2
        for child in range(2):
            rows = slice(child * half, (child + 1) * half)
            got = m["rb", level][:, rows, :].reshape(NEAR * half, RANK)
            hot = jnp.concatenate([hit[rows] for hit in hits], axis=0).astype(BF16)
            hi, lo = [once(piece, hot, 0, 0) for piece in halves(got)]
            gh, gl = halves(hi + lo)
            out = slice(child * RANK, (child + 1) * RANK)
            m[("g", level), "h"][out, :] = gh
            m[("g", level), "l"][out, :] = gl

    def send_up(level, b, u):
        count_tiles, per = tiles_of(level)
        both = times(b, kept(("qw", level)), 0)
        tile = pick(u, m["h", level][...])
        for t in range(count_tiles):
            m["fs", level][t] = jnp.concatenate(
                [both[:, :RANK], both[:, RANK:], tile[:, t * LANES : (t + 1) * LANES]], axis=0
            )
        fs, fa = m["fs", level], m["fa", level]
        fa[near] = fs[near // per]
        fan_near(("fa", level), lambda q: fs.at[q // per], fa)

    def send_on(level):
        n = nb[level + 1]
        arrive(("fa", level))
        fa = m["fa", level]
        tot = jnp.sum(fa[:, : 2 * count, :], axis=0)
        hq = tot[:count] * head[level]
        w = tot[count:] + times(hq, kept(("cross", level)), 0)
        idx = far % n
        wb = m["wb", level]
        wb[idx] = w
        m["tf", level][...] = transposed(fa[:, 2 * count :, :].reshape(NEAR * count, LANES))
        fan(
            n,
            NEAR,
            (("wb", level), lambda q: wb.at[idx], lambda i: wb.at[i], wb.at[pl.ds(0, n - 1)]),
            forward_rows(level, ("tf", level), ("rf", level), ("rf", level)),
        )
        m["hb", level][far % nb[level]] = hq
        spread_own(("hb", level), nb[level], NEAR)

    def receive_up(level):
        n = nb[level + 1]
        half = n // 2
        arrive(("wb", level))
        wb = m["wb", level]
        ws = []
        for child in range(2):
            mc = mask(level, 1)(front[level + 1] * 2 + child)
            ws.append(jnp.sum(wb[child * half : (child + 1) * half], axis=0) * mc)
        inc = -times(jnp.concatenate(ws, axis=1), kept(("g", level)), 0)
        arrive(("rf", level))
        return inc + spread(m["rf", level][...], m["ohf", level][...], NEAR, count)

    def near_sum(name):
        arrive(name)
        return jnp.sum(m[name][...], axis=0)

    saved = {}

    def solve_front(level, local):
        arrive(("hb", level))
        hq = jnp.sum(m["hb", level][...], axis=0)
        z = (local + outer(hq, exp[level][...])) * piv[level][...]
        saved[level] = z
        m["za", level][near] = mult(z, exp[level][...])
        spread_own(("za", level), NEAR, 1)

    def pass_zp(level):
        m["zb", level][far % nb[level]] = near_sum(("za", level))
        spread_own(("zb", level), nb[level], NEAR)

    def base_of(level, zp):
        return outer(saved[level], blk[level][...]) + outer(zp * head[level], q_of(level))

    def tail_of(level, wv):
        qm = q_of(level) * jnp.broadcast_to(head[level][:1], (LANES, RANK))
        keep(("t", level), wv + times(qm, kept(("cross", level)), 0))

    def wv_of(level):
        qh, ql = kept(("qw", level))
        return qh[:, RANK:].astype(F32) + ql[:, RANK:].astype(F32)

    arrive("r0")
    r0 = m["r0"][...]
    lane = lax.broadcasted_iota(jnp.int32, (plane, 2 * LANES), 1).astype(F32)
    at = cap * count
    m["oh0"][...] = jnp.concatenate(
        [(lane == r0[:, at + s : at + s + 1]).astype(F32) for s in range(cap)], axis=1
    ).astype(BF16)
    inc = spread(r0, m["oh0"][...], cap, count)
    b1 = src[1][...] + inc[:, :LANES]
    send_up(1, b1, inc[:, LANES:])

    arrive(("xb", 0))
    m["xg1"][near] = jnp.sum(m["xb", 0][...], axis=0)
    spread_own("xg1", NEAR, 1)
    local1 = mult(b1, blk[1][...])
    saved[0] = z0
    arrive("zx")
    base0 = base_of(0, jnp.sum(m["zx"][...], axis=0))
    build(1)
    arrive("xg1")
    keep(("cross", 1), m["xg1"][...].reshape(RANK, RANK))
    send_on(1)

    arrive(("xb", 1))
    arrive(("xb", 2))
    m["xg2"][near] = jnp.concatenate([jnp.sum(m["xb", j][...], axis=0) for j in (1, 2)], axis=0)
    spread_own("xg2", NEAR, 1)
    tail_of(0, mult(blk[0][...], v_of(0)))
    tail_of(1, wv_of(1))

    inc = receive_up(1)
    b2 = src[2][...] + inc[:, :LANES]
    send_up(2, b2, inc[:, LANES:])

    local2 = mult(b2, blk[2][...])
    arrive("xg2")
    keep(("cross", 2), m["xg2"][:, :slice_rows, :].reshape(RANK, RANK))
    keep(("cross", 3), m["xg2"][:, slice_rows:, :].reshape(RANK, RANK))
    build(2)
    send_on(2)
    solve_front(1, local1)
    tail_of(2, wv_of(2))

    b3 = src[3][...] + receive_up(2)
    both = times(b3, kept(("qw", 3)), 0)
    m["fa", 3][near] = jnp.concatenate([both[:, :RANK], both[:, RANK:]], axis=0)
    spread_own(("fa", 3), NEAR, 1)
    local3 = mult(b3, blk[3][...]) * piv[3][...]
    solve_front(2, local2)
    pass_zp(1)
    tot = near_sum(("fa", 3))
    hq = tot[:count] * head[3]
    rp = tot[count:] + times(hq, kept(("cross", 3)), 0)
    m["fb"][far] = jnp.concatenate([rp, hq], axis=0)
    spread_own("fb", fars, NEAR)
    early = outer(local3, blk[3][...])
    pass_zp(2)
    arrive(("zb", 1))
    base1 = base_of(1, jnp.sum(m["zb", 1][...], axis=0))
    arrive("fb")
    tot = jnp.sum(m["fb"][...], axis=0)
    ends = jnp.concatenate([tot[:count] * head[3], tot[count:]], axis=1)
    x = early + times(ends, kept(("qw", 3)), 1)

    def send_down(level, full):
        count_tiles, per = tiles_of(level)
        sp = times(full, kept(("g", level)), 1)
        tile = pick(full, m["ohg", level][...])
        for t in range(count_tiles):
            m["bs", level][t] = jnp.concatenate(
                [sp[:, :RANK], sp[:, RANK:], tile[:, t * LANES : (t + 1) * LANES]], axis=0
            )
        bs, ba = m["bs", level], m["ba", level]
        ba[near] = bs[near // per]
        fan_near(("ba", level), lambda q: bs.at[q // per], ba)

    def send_further(level):
        n = nb[level + 1]
        half = n // 2
        arrive(("ba", level))
        ba = m["ba", level]
        tot = jnp.sum(ba[:, : 2 * count, :], axis=0)
        two, sb = m["two", level], m["sb", level]
        two[0] = tot[:count]
        two[1] = tot[count:]
        idx = far % n
        sb[idx] = two[idx // half]
        m["td", level][...] = transposed(ba[:, 2 * count :, :].reshape(NEAR * count, LANES))
        fan(
            n,
            NEAR,
            (("sb", level), lambda q: two.at[q // half], lambda i: sb.at[i], sb.at[pl.ds(0, n - 1)]),
            forward_rows(level, ("td", level), ("rd", level), ("rd", level)),
        )

    def receive_down(level, base):
        arrive(("sb", level))
        s = jnp.sum(m["sb", level][...], axis=0) * side[level]
        x = base - times(s, kept(("t", level)), 1)
        arrive(("rd", level))
        xu = spread(m["rd", level][...], m["ohr", level][...], NEAR, count)
        return x, xu

    send_down(2, x)
    outs[3][...] = x
    arrive(("zb", 2))
    base2 = base_of(2, jnp.sum(m["zb", 2][...], axis=0))
    send_further(2)
    x, xu = receive_down(2, base2)
    send_down(1, jnp.concatenate([x, xu], axis=1))
    outs[2][...] = x
    send_further(1)
    x, xu = receive_down(1, base1)
    m["s0b"][...] = leaf_rows((m["oh0"][...], None), diagonal(jnp.concatenate([x, xu], axis=1), cap))
    send_leaf("s0b", "r0b", "r0b")
    outs[1][...] = x
    arrive("r0b")
    rows = stacked(m["r0b"][...].T[: cap * count])
    half = cap * count
    first = once(rows, m["hch"][...], 1, 0)
    second = once(rows[:half], m["hcl"][...], 1, 0)
    s = None
    for g in range(cap):
        lanes = slice(g * RANK, (g + 1) * RANK)
        up, down = slice(g * count, (g + 1) * count), slice(half + g * count, half + (g + 1) * count)
        part = first[up, lanes] + (first[down, lanes] + second[up, lanes])
        s = part if s is None else s + part
    m["xs"][my4] = s
    spread_own("xs", four, 1)
    arrive("xs")
    s = jnp.sum(m["xs"][...], axis=0) * side[0]
    outs[0][...] = base0 - times(s, kept(("t", 0)), 1)

    for name, part in parts.items():
        wait_for(part, send_sem.at[sem_of(name)])


def solution(mesh):
    leaves, across = mesh.shape["leaf"], mesh.shape["grid"]

    def shards(*args):
        levels = [args[8 * i : 8 * i + 8] for i in range(3)]
        root = args[24:30]
        (sl, bl, el, qs, pv, cl, rk, tg) = zip(*levels)
        src = list(sl) + [root[0]]
        blk = list(bl) + [root[1]]
        exp = list(el) + [root[2]]
        bas = list(qs) + [root[3]]
        piv = [v.reshape(1, -1) for v in list(pv) + [root[4]]]
        rnk = [r.T for r in rk] + [root[5]]
        tgt = [t.reshape(1, -1) for t in tg]
        count = src[0].shape[0]
        ups = [t.shape[1] for t in tgt]
        fronts = [r.shape[0] for r in rk] + [root[5].shape[0]]
        size = [leaves * across // f for f in fronts]
        cap = ups[0] // size[1]
        nb = [s // NEAR for s in size]
        for v in src:
            assert v.shape == (NEAR, LANES)
        assert ups[1:] == [LANES, LANES] and cap * (count + 1) <= LANES
        assert size[2] == 2 * size[1] and size[3] == 2 * size[2] and size[1] % NEAR == 0
        assert NEAR * nb[2] == LANES and NEAR * nb[3] == 2 * LANES
        vm = lambda *s: pltpu.VMEM(s, F32)
        bits = lambda *s: pltpu.VMEM(s, BF16)
        piece = RANK // NEAR
        bufs = {
            "f1": vm(size[0], 2 * count, LANES),
            "c0": vm(size[0], RANK, RANK),
            "zx": vm(size[0], count, LANES),
            "xs": vm(size[0], count, LANES),
            "xp": vm(NEAR, 3 * piece, RANK),
            "xra": vm(NEAR, 3 * piece, RANK),
            "xg1": vm(NEAR, piece, RANK),
            "xg2": vm(NEAR, 2 * piece, RANK),
            "lows": vm(2, count, LANES),
            "la": vm(NEAR, count, LANES),
            "tl": vm(LANES, LANES),
            "hch": bits(size[1], cap * RANK),
            "hcl": bits(size[1], cap * RANK),
            "low0": vm(size[1], LANES),
            "oh0": bits(size[1], cap * 2 * LANES),
            "fb": vm(nb[3], 2 * count, LANES),
        }
        for name in ("s0", "r0", "s0b", "r0b"):
            bufs[name] = vm(size[1], LANES)
        for j in range(3):
            bufs["xb", j] = vm(nb[j + 1], piece, RANK)
        for i in range(4):
            for half in "hl":
                bufs[("cross", i), half] = bits(RANK, RANK)
                bufs[("qw", i), half] = bits(LANES, 2 * RANK)
                bufs[("t", i), half] = bits(LANES, RANK)
        bufs["fa", 3] = vm(NEAR, 2 * count, LANES)
        for i in (1, 2):
            n = nb[i + 1]
            wide = 2 * LANES if i == 1 else LANES
            tiles = NEAR * n // LANES
            bufs["h", i] = bits(NEAR * n, LANES)
            bufs["ohr", i] = bits(n, NEAR * LANES)
            bufs["ohf", i] = bits(n, NEAR * wide)
            bufs["ohg", i] = bits(NEAR * n, wide)
            bufs["pa", i] = vm(NEAR, n, RANK)
            bufs["ra", i] = vm(NEAR, n, RANK)
            bufs["rb", i] = vm(NEAR, n, RANK)
            bufs["lb", i] = vm(n, LANES)
            for half in "hl":
                bufs[("g", i), half] = bits(2 * RANK, wide)
            bufs["fs", i] = vm(tiles, 3 * count, LANES)
            bufs["fa", i] = vm(NEAR, 3 * count, LANES)
            bufs["bs", i] = vm(tiles, 3 * count, LANES)
            bufs["ba", i] = vm(NEAR, 3 * count, LANES)
            bufs["tf", i] = vm(LANES, LANES)
            bufs["td", i] = vm(LANES, LANES)
            bufs["rf", i] = vm(n, LANES)
            bufs["rd", i] = vm(n, LANES)
            bufs["wb", i] = vm(n, count, LANES)
            bufs["sb", i] = vm(n, count, LANES)
            bufs["two", i] = vm(2, count, LANES)
            bufs["hb", i] = vm(nb[i], count, LANES)
            bufs["za", i] = vm(NEAR, count, LANES)
            bufs["zb", i] = vm(nb[i], count, LANES)
        scratch = list(bufs.values())
        scratch += [
            pltpu.SemaphoreType.DMA((48,)),
            pltpu.SemaphoreType.DMA((48,)),
            pltpu.SemaphoreType.REGULAR,
        ]
        vspec = pl.BlockSpec(memory_space=pltpu.VMEM)
        sspec = pl.BlockSpec(memory_space=pltpu.SMEM)
        return pl.pallas_call(
            functools.partial(kernel, (leaves, across, size, ups, count, cap), list(bufs)),
            out_shape=[jax.ShapeDtypeStruct(v.shape, F32) for v in src],
            in_specs=[vspec] * 20 + [sspec] * 4 + [vspec] * 6,
            out_specs=[vspec] * 4,
            scratch_shapes=scratch,
            compiler_params=pltpu.CompilerParams(
                collective_id=0, has_side_effects=True, vmem_limit_bytes=60 * 1024 * 1024
            ),
        )(*src, *blk, *exp, *bas, *piv, *rnk, *cl, *tgt)

    spread_axes = ("leaf", "grid")
    level = (P(None, spread_axes), P(spread_axes, None), P(spread_axes, None), P(spread_axes, None), P(spread_axes))
    mid = level + (P(spread_axes, None), P(), P(spread_axes))
    return jax.shard_map(
        shards,
        mesh=mesh,
        in_specs=mid * 3 + level + (P(),),
        out_specs=(P(None, spread_axes),) * 4,
        check_vma=False,
    )
```

time: 316 us -> 108 us (0.34)
  Pallas kernels: 310 us -> 103 us
    pallas_call x1, Pallas kernels: 310 us -> 103 us  [shards(): pl.pallas_call(functools.partial(kernel, (leaves, across, size, ups, coun...]
where the time goes in v1:
time: 108 us
  Pallas kernels  103 us (95%)
  local copies, waits for them, and re-layouts  4.62 us (4%)
    pallas_call x1, Pallas kernels, shards(): pl.pallas_call(functools.partial(kernel, (leaves, across, size, ups, coun...  103 us
    unnamed x15, local copies, waits for them, and re-layouts  4.62 us

profile of v1, /device:TPU:1, one launch (start us, length us, event | category | flops | bytes accessed | tf_op | source)
XLA Modules:
  0.0 108.1 jit_solution(12433061274071326678)
XLA Ops:
  0.6 0.0 copy-start.4
  0.6 0.7 copy-done.4
  1.3 0.6 copy.34
  2.0 102.8 %shard_map.309 = (f32[8,128]{1,0:T(8,128)}, f32[8,128]{1,0:T(8,128)}, f32[8,128]{1,0:T(8,128)}, f32[8,128]{1,0:T(8,128)}) custom-call(f32[8,128]{1,0:T(8,128)} %refs_0_.1, f32[8,128]{1,0:T(8,128)} %refs_1_.1, f32[8,128]{1,0:T(8,128)} %refs_2_.1, f32[8,128]{1,0:T(8,128)} %refs_3_.1, f32[128,128]{1,0:T(8,128)} %refs_4_.1, f32[128,128]{1,0:T(8,128)} %refs_5_.1, ...), custom_call_target="tpu_custom_call" | custom-call | tf_op jit(solution)/shard_map/pallas_call | solution.py:696
  104.8 0.0 copy-start.3
  104.8 0.7 copy-done.3
  105.5 0.0 copy-start.2
  105.5 0.6 copy.39
  106.1 0.1 copy-done.2
  106.2 0.0 copy-start.1
  106.2 0.6 copy.40
  106.8 0.1 copy-done.1
  106.8 0.0 copy-start
  106.8 0.6 copy.41
  107.4 0.1 copy-done
  107.5 0.6 copy.42
Async XLA Ops:
  0.6 0.7 copy-start.4
  104.8 0.7 copy-start.3
  105.5 0.7 copy-start.2
  106.2 0.7 copy-start.1
  106.8 0.7 copy-start

commit v2 on v1

--- a/solution.py
+++ b/solution.py
@@ -10,7 +10,7 @@
 RANK = 128
 LANES = 128
 NEAR = 8
-MESH = pl.DeviceIdType.MESH
+LOGICAL = pl.DeviceIdType.LOGICAL
 F32 = jnp.float32
 BF16 = jnp.bfloat16
 
@@ -97,9 +97,6 @@
     plane = size[1]
     fars = nb[3]
 
-    def where(peer):
-        return (peer // across, peer % across)
-
     def sem_of(name):
         return sems.setdefault(name, len(sems))
 
@@ -109,12 +106,17 @@
             dst_ref=b,
             send_sem=send_sem.at[sem],
             recv_sem=recv_sem.at[sem],
-            device_id=where(peer),
-            device_id_type=MESH,
+            device_id=peer,
+            device_id_type=LOGICAL,
         )
 
     def wait_for(part, sem):
         pltpu.make_async_copy(part, part, sem).wait()
+
+    ring = nb[1]
+
+    def farthest(n):
+        return sorted(range(n), key=lambda d: -min(d, n - d))
 
     def fan(group, stride, *sets):
         idx = me // stride % group
@@ -123,13 +125,36 @@
             sem_of(name)
             parts[name] = part
 
-        def body(k, carry):
-            q = (idx + k) % group
+        def go(q):
             for name, source, dest, part in sets:
                 remote(source(q), dest(idx), sem_of(name), base + q * stride).start()
-            return carry
-
-        lax.fori_loop(1, group, body, 0)
+
+        if stride == NEAR:
+            rows = group // ring
+            for dy in farthest(rows):
+                line = (idx // ring + dy) % rows * ring
+                for dz in farthest(ring):
+                    if dy or dz:
+                        go(line + (idx + dz) % ring)
+        elif group == plane:
+            for dz in farthest(ring)[:-1]:
+                line = (idx // NEAR + dz) % ring * NEAR
+
+                def body(k, carry, line=line):
+                    go(line + k)
+                    return carry
+
+                lax.fori_loop(0, NEAR, body, 0, unroll=True)
+            for k in range(1, NEAR):
+                go(idx // NEAR * NEAR + (idx + k) % NEAR)
+        elif group == NEAR:
+            for dx in farthest(across):
+                for dc in (1, 0):
+                    if dx or dc:
+                        go((idx // across + dc) % 2 * across + (idx + dx) % across)
+        else:
+            for d in farthest(group)[:-1]:
+                go((idx + d) % group)
 
     def arrive(name):
         wait_for(parts[name], recv_sem.at[sem_of(name)])
@@ -148,14 +173,14 @@
     def greet_near(sem):
         def body(k, carry):
             peer = far * NEAR + (near + k) % NEAR
-            pl.semaphore_signal(sem, inc=1, device_id=where(peer), device_id_type=MESH)
+            pl.semaphore_signal(sem, inc=1, device_id=peer, device_id_type=LOGICAL)
             return carry
 
         lax.fori_loop(1, NEAR, body, 0)
 
     def greet_far(k, carry):
         peer = (far + k) % fars * NEAR + near
-        pl.semaphore_signal(barrier, inc=1, device_id=where(peer), device_id_type=MESH)
+        pl.semaphore_signal(barrier, inc=1, device_id=peer, device_id_type=LOGICAL)
         return carry
 
     lax.fori_loop(1, fars, greet_far, 0)
@@ -165,7 +190,7 @@
 
     def mask(level, which):
         def of(front):
-            rank = rnk[level][which, front] if level < 3 else rnk[level][0, which]
+            rank = rnk[level][which, front] if level < 2 else rnk[level][front, which]
             return (col < rank).astype(F32)
 
         return of
@@ -188,7 +213,7 @@
     my4 = me % four
     s0 = src[0][...]
     local0 = mult(s0, blk[0][...])
-    m["f1"][my4] = jnp.concatenate([mult(s0, q_of(0)), mult(local0, v_of(0))], axis=0)
+    m["f1"][my4] = mult(s0, q_of(0))
     m["c0"][my4] = inner(exp[0][...], v_of(0))
 
     slice_rows = RANK // NEAR
@@ -199,7 +224,8 @@
         inner(exp[3][...] * root_piv, exp[3][...]),
     ]
     for j, cross in enumerate(crosses):
-        m["xp"][:, j * slice_rows : (j + 1) * slice_rows, :] = cross.reshape(NEAR, slice_rows, RANK)
+        buf, at = (m["xp1"], 0) if j == 0 else (m["xp2"], (j - 1) * slice_rows)
+        buf[:, at : at + slice_rows, :] = cross.reshape(NEAR, slice_rows, RANK)
 
     def split_targets(level):
         sep = size[level + 1] * LANES
@@ -259,19 +285,18 @@
     pl.semaphore_wait(barrier, NEAR - 1 + fars - 1)
     greet_near(ready)
     spread_own("f1", four, 1)
-    spread_own("c0", four, 1)
 
     def fan_near(name, source, dest):
         fan(NEAR, 1, (name, source, lambda i: dest.at[i], dest.at[pl.ds(0, NEAR - 1)]))
 
-    m["xra"][near] = m["xp"][near]
-    fan_near("xra", lambda q: m["xp"].at[q], m["xra"])
+    def scatter_near(name, source):
+        m[name][near] = m[source][near]
+        fan_near(name, lambda q: m[source].at[q], m[name])
+
+    scatter_near("xr1", "xp1")
     m["la"][near] = m["lows"][near // 4]
     fan_near("la", lambda q: m["lows"].at[q // 4], m["la"])
-    for level in (1, 2):
-        pa, ra = m["pa", level], m["ra", level]
-        ra[near] = pa[near]
-        fan_near(("ra", level), lambda q, pa=pa: pa.at[q], ra)
+    scatter_near(("ra", 1), ("pa", 1))
 
     def keep(name, value):
         hi, lo = halves(value)
@@ -288,12 +313,19 @@
     keep(("qw", 3), jnp.concatenate([q_of(3), wpp], axis=1))
 
     arrive("f1")
-    arrive("c0")
-    cross0 = jnp.sum(m["c0"][...], axis=0)
-    tot = jnp.sum(m["f1"][...], axis=0)
-    hq0 = tot[:count] * head[0]
-    keep(("cross", 0), cross0)
-    w0 = (tot[count:] + times(hq0, kept(("cross", 0)), 0)) * side[0]
+    hq0 = jnp.sum(m["f1"][...], axis=0) * head[0]
+    y0 = local0 + outer(hq0, exp[0][...])
+    m["fv"][my4] = mult(y0, v_of(0))
+    spread_own("fv", four, 1)
+    scatter_near(("ra", 2), ("pa", 2))
+    scatter_near("xr2", "xp2")
+    z0 = y0 * piv[0][...]
+    m["zx"][my4] = mult(z0, exp[0][...])
+    arrive("xr1")
+    m["xb1"][far % ring] = jnp.sum(m["xr1"][...], axis=0)
+    spread_own("xb1", ring, NEAR)
+    arrive("fv")
+    w0 = jnp.sum(m["fv"][...], axis=0) * side[0]
 
     def leaf_rows(a, b):
         ah, al = a
@@ -321,10 +353,6 @@
     pl.semaphore_wait(ready, NEAR - 1)
     send_leaf("s0", "r0", "r0")
 
-    z0 = (local0 + outer(hq0, exp[0][...])) * piv[0][...]
-    m["zx"][my4] = mult(z0, exp[0][...])
-    spread_own("zx", four, 1)
-
     def store_row(buf, i, row):
         buf[pl.ds(i, 1), :] = row
 
@@ -356,17 +384,19 @@
             rb.at[:, pl.ds(0, n - 1)],
         )
 
-    arrive("xra")
-    sums = jnp.sum(m["xra"][...], axis=0)
-    for j, n in enumerate((nb[1], nb[2], nb[3])):
-        m["xb", j][far % n] = sums[j * slice_rows : (j + 1) * slice_rows]
-    spread_own(("xb", 0), nb[1], NEAR)
     arrive("la")
     m["tl"][...] = transposed(m["la"][...].reshape(NEAR * count, LANES))
     for level in (1, 2):
         arrive(("ra", level))
         fan(nb[level + 1], NEAR, forward_rows(level, "tl", ("lb", level), ("lb", level)), couple_set(level))
-        spread_own(("xb", level), nb[level + 1], NEAR)
+    arrive("xr2")
+    m["xb2"][far % ring] = jnp.sum(m["xr2"][...], axis=0)
+    spread_own("xb2", ring, NEAR)
+    arrive("xb1")
+    m["xg1"][near] = jnp.sum(m["xb1"][...], axis=0)
+    spread_own("xg1", NEAR, 1)
+    spread_own("zx", four, 1)
+    spread_own("c0", four, 1)
 
     def build(level):
         n = nb[level + 1]
@@ -402,38 +432,50 @@
         fa[near] = fs[near // per]
         fan_near(("fa", level), lambda q: fs.at[q // per], fa)
 
+    def send_far(level, kind, first, second, tiles):
+        n = nb[level + 1]
+        half = n // 2
+        per = tiles_of(level)[1]
+        idx = far % n
+        table, source, got = m["t" + kind, level], m[kind + "s", level], m[kind + "b", level]
+        table[...] = transposed(tiles[:, 2 * count :, :].reshape(NEAR * count, LANES))
+        source[:half, :count, :] = jnp.broadcast_to(first[None], (half, count, RANK))
+        source[half:, :count, :] = jnp.broadcast_to(second[None], (half, count, RANK))
+        source[:, count, :] = table[pl.ds(pl.multiple_of(near % per * n, 8), n), :]
+        used = pl.ds(0, count + 1)
+        got[idx, : count + 1, :] = source[idx, : count + 1, :]
+        fan(
+            n,
+            NEAR,
+            (
+                (kind, level),
+                lambda q: source.at[q, used],
+                lambda i: got.at[i, used],
+                got.at[pl.ds(0, n - 1), used],
+            ),
+        )
+
     def send_on(level):
-        n = nb[level + 1]
         arrive(("fa", level))
         fa = m["fa", level]
         tot = jnp.sum(fa[:, : 2 * count, :], axis=0)
         hq = tot[:count] * head[level]
         w = tot[count:] + times(hq, kept(("cross", level)), 0)
-        idx = far % n
-        wb = m["wb", level]
-        wb[idx] = w
-        m["tf", level][...] = transposed(fa[:, 2 * count :, :].reshape(NEAR * count, LANES))
-        fan(
-            n,
-            NEAR,
-            (("wb", level), lambda q: wb.at[idx], lambda i: wb.at[i], wb.at[pl.ds(0, n - 1)]),
-            forward_rows(level, ("tf", level), ("rf", level), ("rf", level)),
-        )
+        send_far(level, "w", w, w, fa)
         m["hb", level][far % nb[level]] = hq
         spread_own(("hb", level), nb[level], NEAR)
 
     def receive_up(level):
         n = nb[level + 1]
         half = n // 2
-        arrive(("wb", level))
+        arrive(("w", level))
         wb = m["wb", level]
         ws = []
         for child in range(2):
             mc = mask(level, 1)(front[level + 1] * 2 + child)
-            ws.append(jnp.sum(wb[child * half : (child + 1) * half], axis=0) * mc)
+            ws.append(jnp.sum(wb[child * half : (child + 1) * half, :count, :], axis=0) * mc)
         inc = -times(jnp.concatenate(ws, axis=1), kept(("g", level)), 0)
-        arrive(("rf", level))
-        return inc + spread(m["rf", level][...], m["ohf", level][...], NEAR, count)
+        return inc + spread(wb[:, count, :], m["ohf", level][...], NEAR, count)
 
     def near_sum(name):
         arrive(name)
@@ -475,9 +517,6 @@
     b1 = src[1][...] + inc[:, :LANES]
     send_up(1, b1, inc[:, LANES:])
 
-    arrive(("xb", 0))
-    m["xg1"][near] = jnp.sum(m["xb", 0][...], axis=0)
-    spread_own("xg1", NEAR, 1)
     local1 = mult(b1, blk[1][...])
     saved[0] = z0
     arrive("zx")
@@ -485,13 +524,16 @@
     build(1)
     arrive("xg1")
     keep(("cross", 1), m["xg1"][...].reshape(RANK, RANK))
+    arrive("xb2")
+    m["xy"][me // plane] = jnp.sum(m["xb2"][...], axis=0)
+    spread_own("xy", total_devices // plane, plane)
     send_on(1)
 
-    arrive(("xb", 1))
-    arrive(("xb", 2))
-    m["xg2"][near] = jnp.concatenate([jnp.sum(m["xb", j][...], axis=0) for j in (1, 2)], axis=0)
+    arrive("xy")
+    pair = me // plane // 2 * 2
+    m["xg2"][near, :slice_rows, :] = jnp.sum(m["xy"][pl.ds(pair, 2), :slice_rows, :], axis=0)
+    m["xg2"][near, slice_rows:, :] = jnp.sum(m["xy"][:, slice_rows:, :], axis=0)
     spread_own("xg2", NEAR, 1)
-    tail_of(0, mult(blk[0][...], v_of(0)))
     tail_of(1, wv_of(1))
 
     inc = receive_up(1)
@@ -499,33 +541,36 @@
     send_up(2, b2, inc[:, LANES:])
 
     local2 = mult(b2, blk[2][...])
+    build(2)
     arrive("xg2")
     keep(("cross", 2), m["xg2"][:, :slice_rows, :].reshape(RANK, RANK))
+    send_on(2)
     keep(("cross", 3), m["xg2"][:, slice_rows:, :].reshape(RANK, RANK))
-    build(2)
-    send_on(2)
+    root_qm = q_of(3) * jnp.broadcast_to(head[3][:1], (LANES, RANK))
+    root_t = wv_of(3) + times(root_qm, kept(("cross", 3)), 0)
+    keep(("qt", 3), jnp.concatenate([root_qm, root_t], axis=1))
     solve_front(1, local1)
     tail_of(2, wv_of(2))
 
     b3 = src[3][...] + receive_up(2)
-    both = times(b3, kept(("qw", 3)), 0)
+    both = times(b3, kept(("qt", 3)), 0)
     m["fa", 3][near] = jnp.concatenate([both[:, :RANK], both[:, RANK:]], axis=0)
     spread_own(("fa", 3), NEAR, 1)
     local3 = mult(b3, blk[3][...]) * piv[3][...]
     solve_front(2, local2)
     pass_zp(1)
-    tot = near_sum(("fa", 3))
-    hq = tot[:count] * head[3]
-    rp = tot[count:] + times(hq, kept(("cross", 3)), 0)
-    m["fb"][far] = jnp.concatenate([rp, hq], axis=0)
+    m["fb"][far] = near_sum(("fa", 3))
     spread_own("fb", fars, NEAR)
+    arrive("c0")
+    keep(("cross", 0), jnp.sum(m["c0"][...], axis=0))
+    tail_of(0, mult(blk[0][...], v_of(0)))
     early = outer(local3, blk[3][...])
     pass_zp(2)
     arrive(("zb", 1))
     base1 = base_of(1, jnp.sum(m["zb", 1][...], axis=0))
     arrive("fb")
     tot = jnp.sum(m["fb"][...], axis=0)
-    ends = jnp.concatenate([tot[:count] * head[3], tot[count:]], axis=1)
+    ends = jnp.concatenate([tot[count:] * head[3], tot[:count]], axis=1)
     x = early + times(ends, kept(("qw", 3)), 1)
 
     def send_down(level, full):
@@ -541,30 +586,17 @@
         fan_near(("ba", level), lambda q: bs.at[q // per], ba)
 
     def send_further(level):
-        n = nb[level + 1]
-        half = n // 2
         arrive(("ba", level))
         ba = m["ba", level]
         tot = jnp.sum(ba[:, : 2 * count, :], axis=0)
-        two, sb = m["two", level], m["sb", level]
-        two[0] = tot[:count]
-        two[1] = tot[count:]
-        idx = far % n
-        sb[idx] = two[idx // half]
-        m["td", level][...] = transposed(ba[:, 2 * count :, :].reshape(NEAR * count, LANES))
-        fan(
-            n,
-            NEAR,
-            (("sb", level), lambda q: two.at[q // half], lambda i: sb.at[i], sb.at[pl.ds(0, n - 1)]),
-            forward_rows(level, ("td", level), ("rd", level), ("rd", level)),
-        )
+        send_far(level, "s", tot[:count], tot[count:], ba)
 
     def receive_down(level, base):
-        arrive(("sb", level))
-        s = jnp.sum(m["sb", level][...], axis=0) * side[level]
+        arrive(("s", level))
+        sb = m["sb", level]
+        s = jnp.sum(sb[:, :count, :], axis=0) * side[level]
         x = base - times(s, kept(("t", level)), 1)
-        arrive(("rd", level))
-        xu = spread(m["rd", level][...], m["ohr", level][...], NEAR, count)
+        xu = spread(sb[:, count, :], m["ohr", level][...], NEAR, count)
         return x, xu
 
     send_down(2, x)
@@ -613,7 +645,7 @@
         exp = list(el) + [root[2]]
         bas = list(qs) + [root[3]]
         piv = [v.reshape(1, -1) for v in list(pv) + [root[4]]]
-        rnk = [r.T for r in rk] + [root[5]]
+        rnk = [rk[0].T, rk[1].T, rk[2], root[5]]
         tgt = [t.reshape(1, -1) for t in tg]
         count = src[0].shape[0]
         ups = [t.shape[1] for t in tgt]
@@ -624,18 +656,25 @@
         for v in src:
             assert v.shape == (NEAR, LANES)
         assert ups[1:] == [LANES, LANES] and cap * (count + 1) <= LANES
+        assert nb[1] == 8 and across == 4 and size[0] == across
         assert size[2] == 2 * size[1] and size[3] == 2 * size[2] and size[1] % NEAR == 0
         assert NEAR * nb[2] == LANES and NEAR * nb[3] == 2 * LANES
         vm = lambda *s: pltpu.VMEM(s, F32)
         bits = lambda *s: pltpu.VMEM(s, BF16)
         piece = RANK // NEAR
         bufs = {
-            "f1": vm(size[0], 2 * count, LANES),
+            "f1": vm(size[0], count, LANES),
+            "fv": vm(size[0], count, LANES),
             "c0": vm(size[0], RANK, RANK),
             "zx": vm(size[0], count, LANES),
             "xs": vm(size[0], count, LANES),
-            "xp": vm(NEAR, 3 * piece, RANK),
-            "xra": vm(NEAR, 3 * piece, RANK),
+            "xp1": vm(NEAR, piece, RANK),
+            "xr1": vm(NEAR, piece, RANK),
+            "xp2": vm(NEAR, 2 * piece, RANK),
+            "xr2": vm(NEAR, 2 * piece, RANK),
+            "xb1": vm(nb[1], piece, RANK),
+            "xb2": vm(nb[1], 2 * piece, RANK),
+            "xy": vm(nb[3] // nb[1], 2 * piece, RANK),
             "xg1": vm(NEAR, piece, RANK),
             "xg2": vm(NEAR, 2 * piece, RANK),
             "lows": vm(2, count, LANES),
@@ -649,13 +688,12 @@
         }
         for name in ("s0", "r0", "s0b", "r0b"):
             bufs[name] = vm(size[1], LANES)
-        for j in range(3):
-            bufs["xb", j] = vm(nb[j + 1], piece, RANK)
         for i in range(4):
             for half in "hl":
                 bufs[("cross", i), half] = bits(RANK, RANK)
                 bufs[("qw", i), half] = bits(LANES, 2 * RANK)
                 bufs[("t", i), half] = bits(LANES, RANK)
+                bufs[("qt", i), half] = bits(LANES, 2 * RANK)
         bufs["fa", 3] = vm(NEAR, 2 * count, LANES)
         for i in (1, 2):
             n = nb[i + 1]
@@ -675,13 +713,10 @@
             bufs["fa", i] = vm(NEAR, 3 * count, LANES)
             bufs["bs", i] = vm(tiles, 3 * count, LANES)
             bufs["ba", i] = vm(NEAR, 3 * count, LANES)
-            bufs["tf", i] = vm(LANES, LANES)
-            bufs["td", i] = vm(LANES, LANES)
-            bufs["rf", i] = vm(n, LANES)
-            bufs["rd", i] = vm(n, LANES)
-            bufs["wb", i] = vm(n, count, LANES)
-            bufs["sb", i] = vm(n, count, LANES)
-            bufs["two", i] = vm(2, count, LANES)
+            for kind in "ws":
+                bufs["t" + kind, i] = vm(LANES, LANES)
+                bufs[kind + "s", i] = vm(n, 2 * count, LANES)
+                bufs[kind + "b", i] = vm(n, 2 * count, LANES)
             bufs["hb", i] = vm(nb[i], count, LANES)
             bufs["za", i] = vm(NEAR, count, LANES)
             bufs["zb", i] = vm(nb[i], count, LANES)

time: 108 us -> 95.2 us (0.88)
  Pallas kernels: 103 us -> 91 us
  local copies, waits for them, and re-layouts: 4.62 us -> 3.3 us
    pallas_call x1, Pallas kernels: 103 us -> 91 us  [shards(): pl.pallas_call(functools.partial(kernel, (leaves, across, size, ups, coun...]
    unnamed x15 -> x12, local copies, waits for them, and re-layouts: 4.62 us -> 3.3 us
where the time goes in v2:
time: 95.2 us; the launch traced here: 95 us
  Pallas kernels  91 us (96%)
  local copies, waits for them, and re-layouts  3.3 us (3%)
    pallas_call x1, Pallas kernels, shards(): pl.pallas_call(functools.partial(kernel, (leaves, across, size, ups, coun...  91 us
    unnamed x12, local copies, waits for them, and re-layouts  3.3 us

profile of v2, /device:TPU:1, one launch (start us, length us, event | category | flops | bytes accessed | tf_op | source)
XLA Modules:
  0.0 95.0 jit_solution(13551445099675226088)
XLA Ops:
  0.6 91.0 %shard_map.309 = (f32[8,128]{1,0:T(8,128)}, f32[8,128]{1,0:T(8,128)}, f32[8,128]{1,0:T(8,128)}, f32[8,128]{1,0:T(8,128)}) custom-call(f32[8,128]{1,0:T(8,128)} %refs_0_.1, f32[8,128]{1,0:T(8,128)} %refs_1_.1, f32[8,128]{1,0:T(8,128)} %refs_2_.1, f32[8,128]{1,0:T(8,128)} %refs_3_.1, f32[128,128]{1,0:T(8,128)} %refs_4_.1, f32[128,128]{1,0:T(8,128)} %refs_5_.1, ...), custom_call_target="tpu_custom_call" | custom-call | tf_op jit(solution)/shard_map/pallas_call | solution.py:731
  91.7 0.0 copy-start.3
  91.7 0.7 copy-done.3
  92.4 0.0 copy-start.2
  92.4 0.6 copy.38
  93.0 0.1 copy-done.2
  93.0 0.0 copy-start.1
  93.0 0.6 copy.39
  93.6 0.1 copy-done.1
  93.7 0.0 copy-start
  93.7 0.6 copy.40
  94.3 0.1 copy-done
  94.4 0.6 copy.41
Async XLA Ops:
  91.7 0.7 copy-start.3
  92.4 0.7 copy-start.2
  93.0 0.7 copy-start.1
  93.7 0.7 copy-start

commit v3 on v2

--- a/solution.py
+++ b/solution.py
@@ -68,25 +68,30 @@
     return out
 
 
-def diagonal(x, groups):
+def diagonal(x, groups, again=1):
     count, wide = x.shape
     zero = jnp.zeros((count, wide), F32)
     rows = [
         jnp.concatenate([x if h == g else zero for h in range(groups)], axis=1) for g in range(groups)
     ]
-    rows.append(jnp.zeros((LANES - groups * count, groups * wide), F32))
+    rows = rows * again
+    left = LANES - len(rows) * count
+    if left:
+        rows.append(jnp.zeros((left, groups * wide), F32))
     return jnp.concatenate(rows, axis=0)
 
 
 def kernel(cfg, names, *refs):
     leaves, across, size, ups, count, cap = cfg
     total_devices = leaves * across
-    (src, blk, exp, bas, piv, rnk) = [refs[4 * i : 4 * i + 4] for i in range(6)]
-    cpl = refs[24:27]
-    tgt = refs[27:30]
-    outs = refs[30:34]
-    m = dict(zip(names, refs[34:-3]))
-    send_sem, recv_sem, ready = refs[-3:]
+    given, rnk, out = refs[:26], refs[26:30], refs[30]
+    outs = [out.at[pl.ds(i * count, count)] for i in range(4)]
+    m = dict(zip(names, refs[31:-4]))
+    send_sem, recv_sem, load_sem, ready = refs[-4:]
+    held = [m["in", i] for i in range(26)]
+    (src, blk, exp, bas, piv) = [held[4 * i : 4 * i + 4] for i in range(5)]
+    cpl, tgt = held[20:23], held[23:26]
+    loads = [pltpu.make_async_copy(given[i], held[i], load_sem.at[i]) for i in range(26)]
     sems = {}
     parts = {}
 
@@ -185,6 +190,10 @@
 
     lax.fori_loop(1, fars, greet_far, 0)
     greet_near(barrier)
+    soon = (0, 12)
+    rest = [i for i in range(26) if i not in soon]
+    for i in soon + tuple(rest):
+        loads[i].start()
 
     col = lax.broadcasted_iota(jnp.int32, (count, RANK), 1)
 
@@ -211,9 +220,16 @@
 
     four = size[0]
     my4 = me % four
+    for i in soon:
+        loads[i].wait()
     s0 = src[0][...]
+    m["f1"][my4] = mult(s0, q_of(0))
+    pl.semaphore_wait(barrier, NEAR - 1 + fars - 1)
+    greet_near(ready)
+    spread_own("f1", four, 1)
+    for i in rest:
+        loads[i].wait()
     local0 = mult(s0, blk[0][...])
-    m["f1"][my4] = mult(s0, q_of(0))
     m["c0"][my4] = inner(exp[0][...], v_of(0))
 
     slice_rows = RANK // NEAR
@@ -252,8 +268,10 @@
             si = lax.broadcasted_iota(jnp.int32, (plane, u), 0) + s * plane
             hit = (si == slot).astype(F32).astype(BF16)
             lanes = slice(s * RANK, (s + 1) * RANK)
-            m["hch"][:, lanes] = once(hit, ch, 1, 0).astype(BF16)
-            m["hcl"][:, lanes] = once(hit, cl, 1, 0).astype(BF16)
+            high, low_part = once(hit, ch, 1, 0), once(hit, cl, 1, 0)
+            m["hch"][:, lanes] = high.astype(BF16)
+            m["hcl"][:, lanes] = low_part.astype(BF16)
+            m["hx"][my4, s * plane : (s + 1) * plane, :] = high + low_part
             mine = jnp.where(li == cap * count + s, low.astype(F32), 0.0).astype(BF16)
             part = once(hit, mine, 1, 1)
             lowmat = part if lowmat is None else lowmat + part
@@ -282,10 +300,6 @@
         m["lows"][t] = jnp.where(ri == 0, two, jnp.where(ri == 1, low1, 0.0))
     pack_leaf()
 
-    pl.semaphore_wait(barrier, NEAR - 1 + fars - 1)
-    greet_near(ready)
-    spread_own("f1", four, 1)
-
     def fan_near(name, source, dest):
         fan(NEAR, 1, (name, source, lambda i: dest.at[i], dest.at[pl.ds(0, NEAR - 1)]))
 
@@ -335,14 +349,14 @@
 
     place = me % plane
 
-    def send_leaf(rows, got, name):
-        m[got][pl.ds(place, 1), :] = m[rows][pl.ds(place, 1), :]
+    def send_leaf(rows, got, row):
+        m[got][pl.ds(place, 1), :] = m[rows][pl.ds(row(place), 1), :]
         fan(
             plane,
             1,
             (
-                name,
-                lambda q: m[rows].at[pl.ds(q, 1)],
+                got,
+                lambda q: m[rows].at[pl.ds(row(q), 1)],
                 lambda i: m[got].at[pl.ds(i, 1)],
                 m[got].at[pl.ds(0, plane - 1)],
             ),
@@ -351,7 +365,7 @@
     hc = (m["hch"][...], m["hcl"][...])
     m["s0"][...] = leaf_rows(hc, diagonal(-w0, cap)) + m["low0"][...]
     pl.semaphore_wait(ready, NEAR - 1)
-    send_leaf("s0", "r0", "r0")
+    send_leaf("s0", "r0", lambda q: q)
 
     def store_row(buf, i, row):
         buf[pl.ds(i, 1), :] = row
@@ -545,6 +559,7 @@
     arrive("xg2")
     keep(("cross", 2), m["xg2"][:, :slice_rows, :].reshape(RANK, RANK))
     send_on(2)
+    spread_own("hx", four, 1)
     keep(("cross", 3), m["xg2"][:, slice_rows:, :].reshape(RANK, RANK))
     root_qm = q_of(3) * jnp.broadcast_to(head[3][:1], (LANES, RANK))
     root_t = wv_of(3) + times(root_qm, kept(("cross", 3)), 0)
@@ -554,8 +569,11 @@
 
     b3 = src[3][...] + receive_up(2)
     both = times(b3, kept(("qt", 3)), 0)
-    m["fa", 3][near] = jnp.concatenate([both[:, :RANK], both[:, RANK:]], axis=0)
-    spread_own(("fa", 3), NEAR, 1)
+    core = near // across
+    m["fs3"][0] = both[:, :RANK]
+    m["fs3"][1] = both[:, RANK:]
+    m["fa", 3][near] = m["fs3"][core]
+    fan_near(("fa", 3), lambda q: m["fs3"].at[q // across], m["fa", 3])
     local3 = mult(b3, blk[3][...]) * piv[3][...]
     solve_front(2, local2)
     pass_zp(1)
@@ -564,13 +582,19 @@
     arrive("c0")
     keep(("cross", 0), jnp.sum(m["c0"][...], axis=0))
     tail_of(0, mult(blk[0][...], v_of(0)))
+    arrive("hx")
+    for k in range(four):
+        at = slice(k * cap * plane, (k + 1) * cap * plane)
+        m["hxh"][at, :], m["hxl"][at, :] = halves(m["hx"][k])
     early = outer(local3, blk[3][...])
     pass_zp(2)
     arrive(("zb", 1))
     base1 = base_of(1, jnp.sum(m["zb", 1][...], axis=0))
     arrive("fb")
-    tot = jnp.sum(m["fb"][...], axis=0)
-    ends = jnp.concatenate([tot[count:] * head[3], tot[:count]], axis=1)
+    m["fc"][core] = jnp.sum(m["fb"][...], axis=0)
+    spread_own("fc", 2, across)
+    arrive("fc")
+    ends = jnp.concatenate([m["fc"][1] * head[3], m["fc"][0]], axis=1)
     x = early + times(ends, kept(("qw", 3)), 1)
 
     def send_down(level, full):
@@ -609,24 +633,20 @@
     outs[2][...] = x
     send_further(1)
     x, xu = receive_down(1, base1)
-    m["s0b"][...] = leaf_rows((m["oh0"][...], None), diagonal(jnp.concatenate([x, xu], axis=1), cap))
-    send_leaf("s0b", "r0b", "r0b")
+    full = diagonal(jnp.concatenate([x, xu], axis=1), cap, four)
+    rows = leaf_rows((m["oh0"][...], None), full)
+    ri = lax.broadcasted_iota(jnp.int32, (plane, LANES), 0)
+    li = lax.broadcasted_iota(jnp.int32, (plane, LANES), 1)
+    rows = jnp.where(li // (cap * count) == ri % four, rows, 0.0)
+    rows = rows + pltpu.roll(rows, plane - 1, 0)
+    m["s0b"][...] = rows + pltpu.roll(rows, plane - 2, 0)
+    send_leaf("s0b", "r0b", lambda q: q // four * four)
     outs[1][...] = x
     arrive("r0b")
-    rows = stacked(m["r0b"][...].T[: cap * count])
-    half = cap * count
-    first = once(rows, m["hch"][...], 1, 0)
-    second = once(rows[:half], m["hcl"][...], 1, 0)
-    s = None
-    for g in range(cap):
-        lanes = slice(g * RANK, (g + 1) * RANK)
-        up, down = slice(g * count, (g + 1) * count), slice(half + g * count, half + (g + 1) * count)
-        part = first[up, lanes] + (first[down, lanes] + second[up, lanes])
-        s = part if s is None else s + part
-    m["xs"][my4] = s
-    spread_own("xs", four, 1)
-    arrive("xs")
-    s = jnp.sum(m["xs"][...], axis=0) * side[0]
+    rows = transposed(m["r0b"][...])
+    pieces = [rows[g * count : (g + 1) * count] for g in range(four * cap)]
+    pairs = [pieces[2 * g] + pltpu.roll(pieces[2 * g + 1], plane, 1) for g in range(four * cap // 2)]
+    s = times(jnp.concatenate(pairs, axis=1), (m["hxh"][...], m["hxl"][...]), 0) * side[0]
     outs[0][...] = base0 - times(s, kept(("t", 0)), 1)
 
     for name, part in parts.items():
@@ -656,6 +676,7 @@
         for v in src:
             assert v.shape == (NEAR, LANES)
         assert ups[1:] == [LANES, LANES] and cap * (count + 1) <= LANES
+        assert 2 * size[1] == LANES and size[0] * cap * count == LANES
         assert nb[1] == 8 and across == 4 and size[0] == across
         assert size[2] == 2 * size[1] and size[3] == 2 * size[2] and size[1] % NEAR == 0
         assert NEAR * nb[2] == LANES and NEAR * nb[3] == 2 * LANES
@@ -667,7 +688,6 @@
             "fv": vm(size[0], count, LANES),
             "c0": vm(size[0], RANK, RANK),
             "zx": vm(size[0], count, LANES),
-            "xs": vm(size[0], count, LANES),
             "xp1": vm(NEAR, piece, RANK),
             "xr1": vm(NEAR, piece, RANK),
             "xp2": vm(NEAR, 2 * piece, RANK),
@@ -684,7 +704,12 @@
             "hcl": bits(size[1], cap * RANK),
             "low0": vm(size[1], LANES),
             "oh0": bits(size[1], cap * 2 * LANES),
-            "fb": vm(nb[3], 2 * count, LANES),
+            "fb": vm(nb[3], count, LANES),
+            "fs3": vm(2, count, LANES),
+            "fc": vm(2, count, LANES),
+            "hx": vm(size[0], cap * size[1], RANK),
+            "hxh": bits(size[0] * cap * size[1], RANK),
+            "hxl": bits(size[0] * cap * size[1], RANK),
         }
         for name in ("s0", "r0", "s0b", "r0b"):
             bufs[name] = vm(size[1], LANES)
@@ -694,7 +719,7 @@
                 bufs[("qw", i), half] = bits(LANES, 2 * RANK)
                 bufs[("t", i), half] = bits(LANES, RANK)
                 bufs[("qt", i), half] = bits(LANES, 2 * RANK)
-        bufs["fa", 3] = vm(NEAR, 2 * count, LANES)
+        bufs["fa", 3] = vm(NEAR, count, LANES)
         for i in (1, 2):
             n = nb[i + 1]
             wide = 2 * LANES if i == 1 else LANES
@@ -720,24 +745,29 @@
             bufs["hb", i] = vm(nb[i], count, LANES)
             bufs["za", i] = vm(NEAR, count, LANES)
             bufs["zb", i] = vm(nb[i], count, LANES)
+        arrays = [*src, *blk, *exp, *bas, *piv, *cl, *tgt]
+        for i, v in enumerate(arrays):
+            bufs["in", i] = pltpu.VMEM(v.shape, v.dtype)
         scratch = list(bufs.values())
         scratch += [
             pltpu.SemaphoreType.DMA((48,)),
             pltpu.SemaphoreType.DMA((48,)),
+            pltpu.SemaphoreType.DMA((26,)),
             pltpu.SemaphoreType.REGULAR,
         ]
         vspec = pl.BlockSpec(memory_space=pltpu.VMEM)
         sspec = pl.BlockSpec(memory_space=pltpu.SMEM)
-        return pl.pallas_call(
+        whole = pl.pallas_call(
             functools.partial(kernel, (leaves, across, size, ups, count, cap), list(bufs)),
-            out_shape=[jax.ShapeDtypeStruct(v.shape, F32) for v in src],
-            in_specs=[vspec] * 20 + [sspec] * 4 + [vspec] * 6,
-            out_specs=[vspec] * 4,
+            out_shape=jax.ShapeDtypeStruct((4 * count, LANES), F32),
+            in_specs=[pl.BlockSpec(memory_space=pl.ANY)] * 26 + [sspec] * 4,
+            out_specs=vspec,
             scratch_shapes=scratch,
             compiler_params=pltpu.CompilerParams(
                 collective_id=0, has_side_effects=True, vmem_limit_bytes=60 * 1024 * 1024
             ),
-        )(*src, *blk, *exp, *bas, *piv, *rnk, *cl, *tgt)
+        )(*arrays, *rnk)
+        return tuple(whole[i * count : (i + 1) * count] for i in range(4))
 
     spread_axes = ("leaf", "grid")
     level = (P(None, spread_axes), P(spread_axes, None), P(spread_axes, None), P(spread_axes, None), P(spread_axes))

time: 95.2 us -> 88.8 us (0.933)
  Pallas kernels: 91 us -> 86.7 us
  local copies, waits for them, and re-layouts: 3.3 us -> 1.3 us
    pallas_call x1, Pallas kernels: 91 us -> 86.7 us  [shards(): pl.pallas_call(functools.partial(kernel, (leaves, across, size, ups, coun...]
    unnamed x12 -> x0, local copies, waits for them, and re-layouts: 3.3 us -> none
    slice x0 -> x1, local copies, waits for them, and re-layouts: none -> 1.3 us  [shards(): return tuple((whole[i * count:(i + 1) * count] for i in range(4)))]
where the time goes in v3:
time: 88.8 us; the launch traced here: 88.6 us
  Pallas kernels  86.7 us (98%)
  local copies, waits for them, and re-layouts  1.3 us (1%)
    pallas_call x1, Pallas kernels, shards(): pl.pallas_call(functools.partial(kernel, (leaves, across, size, ups, coun...  86.7 us

profile of v3, /device:TPU:1, one launch (start us, length us, event | category | flops | bytes accessed | tf_op | source)
XLA Modules:
  0.0 88.6 jit_solution(8829344108609671113)
XLA Ops:
  0.6 86.7 %shard_map.309 = f32[32,128]{1,0:T(8,128)} custom-call(f32[8,128]{1,0:T(8,128)} %refs_0_.1, f32[8,128]{1,0:T(8,128)} %refs_1_.1, f32[8,128]{1,0:T(8,128)} %refs_2_.1, f32[8,128]{1,0:T(8,128)} %refs_3_.1, f32[128,128]{1,0:T(8,128)} %refs_4_.1, f32[128,128]{1,0:T(8,128)} %refs_5_.1, f32[128,128]{1,0:T(8,128)} %refs_6_.1, f32[128,128]{1,0:T(8,128)} %refs_7_.1, ...), custom_call_target="tpu_custom_call" | custom-call | tf_op jit(solution)/shard_map/pallas_call | solution.py:760
  87.3 1.3 %fusion = (f32[8,128]{1,0:T(8,128)}, f32[8,128]{1,0:T(8,128)}, f32[8,128]{1,0:T(8,128)}, f32[8,128]{1,0:T(8,128)}) fusion(f32[32,128]{1,0:T(8,128)} %shard_map.309), kind=kLoop, calls=%fused_computation | loop fusion | bytes 32768 | tf_op jit(solution)/shard_map/slice | solution.py:770

commit v4 on v3

--- a/solution.py
+++ b/solution.py
@@ -84,14 +84,15 @@
 def kernel(cfg, names, *refs):
     leaves, across, size, ups, count, cap = cfg
     total_devices = leaves * across
-    given, rnk, out = refs[:26], refs[26:30], refs[30]
+    count_in = 30
+    given, out = refs[:count_in], refs[count_in]
     outs = [out.at[pl.ds(i * count, count)] for i in range(4)]
-    m = dict(zip(names, refs[31:-4]))
+    m = dict(zip(names, refs[count_in + 1 : -4]))
     send_sem, recv_sem, load_sem, ready = refs[-4:]
-    held = [m["in", i] for i in range(26)]
+    held = [m["in", i] for i in range(count_in)]
     (src, blk, exp, bas, piv) = [held[4 * i : 4 * i + 4] for i in range(5)]
-    cpl, tgt = held[20:23], held[23:26]
-    loads = [pltpu.make_async_copy(given[i], held[i], load_sem.at[i]) for i in range(26)]
+    cpl, tgt, rnk = held[20:23], held[23:26], held[26:30]
+    loads = [pltpu.make_async_copy(given[i], held[i], load_sem.at[i]) for i in range(count_in)]
     sems = {}
     parts = {}
 
@@ -191,22 +192,18 @@
     lax.fori_loop(1, fars, greet_far, 0)
     greet_near(barrier)
     soon = (0, 12)
-    rest = [i for i in range(26) if i not in soon]
+    rest = [i for i in range(count_in) if i not in soon]
     for i in soon + tuple(rest):
         loads[i].start()
 
-    col = lax.broadcasted_iota(jnp.int32, (count, RANK), 1)
-
-    def mask(level, which):
-        def of(front):
-            rank = rnk[level][which, front] if level < 2 else rnk[level][front, which]
-            return (col < rank).astype(F32)
-
-        return of
-
-    front = [me // s for s in size]
-    head = [mask(level, 0)(front[level]) for level in range(4)]
-    side = [mask(level, 1)(front[level]) for level in range(3)]
+    def mask(level, which, front):
+        ranks = rnk[level][...].astype(F32)
+        axis = 1 if level < 2 else 0
+        line = ranks[which : which + 1, :] if level < 2 else ranks[:, which : which + 1]
+        here = lax.broadcasted_iota(jnp.int32, line.shape, axis) == front
+        rank = jnp.sum(jnp.where(here, line, 0.0), axis=axis, keepdims=True)
+        col = lax.broadcasted_iota(jnp.int32, (count, RANK), 1).astype(F32)
+        return (col < rank).astype(F32)
 
     def q_of(level):
         return bas[level][:, :RANK]
@@ -229,6 +226,12 @@
     spread_own("f1", four, 1)
     for i in rest:
         loads[i].wait()
+    front = [me // n for n in size]
+    head = [mask(level, 0, front[level]) for level in range(4)]
+    side = [mask(level, 1, front[level]) for level in range(3)]
+    below = [None] + [
+        [mask(level, 1, front[level + 1] * 2 + child) for child in range(2)] for level in (1, 2)
+    ]
     local0 = mult(s0, blk[0][...])
     m["c0"][my4] = inner(exp[0][...], v_of(0))
 
@@ -446,16 +449,20 @@
         fa[near] = fs[near // per]
         fan_near(("fa", level), lambda q: fs.at[q // per], fa)
 
-    def send_far(level, kind, first, second, tiles):
+    def rows_of(level, kind, tiles):
+        n = nb[level + 1]
+        table = m["t" + kind, level]
+        table[...] = transposed(tiles.reshape(NEAR * count, LANES))
+        return table[pl.ds(pl.multiple_of(near % tiles_of(level)[1] * n, 8), n), :]
+
+    def send_far(level, kind, first, second, rows):
         n = nb[level + 1]
         half = n // 2
-        per = tiles_of(level)[1]
         idx = far % n
-        table, source, got = m["t" + kind, level], m[kind + "s", level], m[kind + "b", level]
-        table[...] = transposed(tiles[:, 2 * count :, :].reshape(NEAR * count, LANES))
+        source, got = m[kind + "s", level], m[kind + "b", level]
         source[:half, :count, :] = jnp.broadcast_to(first[None], (half, count, RANK))
         source[half:, :count, :] = jnp.broadcast_to(second[None], (half, count, RANK))
-        source[:, count, :] = table[pl.ds(pl.multiple_of(near % per * n, 8), n), :]
+        source[:, count, :] = rows
         used = pl.ds(0, count + 1)
         got[idx, : count + 1, :] = source[idx, : count + 1, :]
         fan(
@@ -475,7 +482,7 @@
         tot = jnp.sum(fa[:, : 2 * count, :], axis=0)
         hq = tot[:count] * head[level]
         w = tot[count:] + times(hq, kept(("cross", level)), 0)
-        send_far(level, "w", w, w, fa)
+        send_far(level, "w", w, w, rows_of(level, "w", fa[:, 2 * count :, :]))
         m["hb", level][far % nb[level]] = hq
         spread_own(("hb", level), nb[level], NEAR)
 
@@ -486,7 +493,7 @@
         wb = m["wb", level]
         ws = []
         for child in range(2):
-            mc = mask(level, 1)(front[level + 1] * 2 + child)
+            mc = below[level][child]
             ws.append(jnp.sum(wb[child * half : (child + 1) * half, :count, :], axis=0) * mc)
         inc = -times(jnp.concatenate(ws, axis=1), kept(("g", level)), 0)
         return inc + spread(wb[:, count, :], m["ohf", level][...], NEAR, count)
@@ -494,108 +501,6 @@
     def near_sum(name):
         arrive(name)
         return jnp.sum(m[name][...], axis=0)
-
-    saved = {}
-
-    def solve_front(level, local):
-        arrive(("hb", level))
-        hq = jnp.sum(m["hb", level][...], axis=0)
-        z = (local + outer(hq, exp[level][...])) * piv[level][...]
-        saved[level] = z
-        m["za", level][near] = mult(z, exp[level][...])
-        spread_own(("za", level), NEAR, 1)
-
-    def pass_zp(level):
-        m["zb", level][far % nb[level]] = near_sum(("za", level))
-        spread_own(("zb", level), nb[level], NEAR)
-
-    def base_of(level, zp):
-        return outer(saved[level], blk[level][...]) + outer(zp * head[level], q_of(level))
-
-    def tail_of(level, wv):
-        qm = q_of(level) * jnp.broadcast_to(head[level][:1], (LANES, RANK))
-        keep(("t", level), wv + times(qm, kept(("cross", level)), 0))
-
-    def wv_of(level):
-        qh, ql = kept(("qw", level))
-        return qh[:, RANK:].astype(F32) + ql[:, RANK:].astype(F32)
-
-    arrive("r0")
-    r0 = m["r0"][...]
-    lane = lax.broadcasted_iota(jnp.int32, (plane, 2 * LANES), 1).astype(F32)
-    at = cap * count
-    m["oh0"][...] = jnp.concatenate(
-        [(lane == r0[:, at + s : at + s + 1]).astype(F32) for s in range(cap)], axis=1
-    ).astype(BF16)
-    inc = spread(r0, m["oh0"][...], cap, count)
-    b1 = src[1][...] + inc[:, :LANES]
-    send_up(1, b1, inc[:, LANES:])
-
-    local1 = mult(b1, blk[1][...])
-    saved[0] = z0
-    arrive("zx")
-    base0 = base_of(0, jnp.sum(m["zx"][...], axis=0))
-    build(1)
-    arrive("xg1")
-    keep(("cross", 1), m["xg1"][...].reshape(RANK, RANK))
-    arrive("xb2")
-    m["xy"][me // plane] = jnp.sum(m["xb2"][...], axis=0)
-    spread_own("xy", total_devices // plane, plane)
-    send_on(1)
-
-    arrive("xy")
-    pair = me // plane // 2 * 2
-    m["xg2"][near, :slice_rows, :] = jnp.sum(m["xy"][pl.ds(pair, 2), :slice_rows, :], axis=0)
-    m["xg2"][near, slice_rows:, :] = jnp.sum(m["xy"][:, slice_rows:, :], axis=0)
-    spread_own("xg2", NEAR, 1)
-    tail_of(1, wv_of(1))
-
-    inc = receive_up(1)
-    b2 = src[2][...] + inc[:, :LANES]
-    send_up(2, b2, inc[:, LANES:])
-
-    local2 = mult(b2, blk[2][...])
-    build(2)
-    arrive("xg2")
-    keep(("cross", 2), m["xg2"][:, :slice_rows, :].reshape(RANK, RANK))
-    send_on(2)
-    spread_own("hx", four, 1)
-    keep(("cross", 3), m["xg2"][:, slice_rows:, :].reshape(RANK, RANK))
-    root_qm = q_of(3) * jnp.broadcast_to(head[3][:1], (LANES, RANK))
-    root_t = wv_of(3) + times(root_qm, kept(("cross", 3)), 0)
-    keep(("qt", 3), jnp.concatenate([root_qm, root_t], axis=1))
-    solve_front(1, local1)
-    tail_of(2, wv_of(2))
-
-    b3 = src[3][...] + receive_up(2)
-    both = times(b3, kept(("qt", 3)), 0)
-    core = near // across
-    m["fs3"][0] = both[:, :RANK]
-    m["fs3"][1] = both[:, RANK:]
-    m["fa", 3][near] = m["fs3"][core]
-    fan_near(("fa", 3), lambda q: m["fs3"].at[q // across], m["fa", 3])
-    local3 = mult(b3, blk[3][...]) * piv[3][...]
-    solve_front(2, local2)
-    pass_zp(1)
-    m["fb"][far] = near_sum(("fa", 3))
-    spread_own("fb", fars, NEAR)
-    arrive("c0")
-    keep(("cross", 0), jnp.sum(m["c0"][...], axis=0))
-    tail_of(0, mult(blk[0][...], v_of(0)))
-    arrive("hx")
-    for k in range(four):
-        at = slice(k * cap * plane, (k + 1) * cap * plane)
-        m["hxh"][at, :], m["hxl"][at, :] = halves(m["hx"][k])
-    early = outer(local3, blk[3][...])
-    pass_zp(2)
-    arrive(("zb", 1))
-    base1 = base_of(1, jnp.sum(m["zb", 1][...], axis=0))
-    arrive("fb")
-    m["fc"][core] = jnp.sum(m["fb"][...], axis=0)
-    spread_own("fc", 2, across)
-    arrive("fc")
-    ends = jnp.concatenate([m["fc"][1] * head[3], m["fc"][0]], axis=1)
-    x = early + times(ends, kept(("qw", 3)), 1)
 
     def send_down(level, full):
         count_tiles, per = tiles_of(level)
@@ -613,7 +518,7 @@
         arrive(("ba", level))
         ba = m["ba", level]
         tot = jnp.sum(ba[:, : 2 * count, :], axis=0)
-        send_far(level, "s", tot[:count], tot[count:], ba)
+        send_far(level, "s", tot[:count], tot[count:], rows_of(level, "s", ba[:, 2 * count :, :]))
 
     def receive_down(level, base):
         arrive(("s", level))
@@ -623,15 +528,140 @@
         xu = spread(sb[:, count, :], m["ohr", level][...], NEAR, count)
         return x, xu
 
-    send_down(2, x)
-    outs[3][...] = x
+    saved = {}
+
+    def solve_front(level, local):
+        arrive(("hb", level))
+        hq = jnp.sum(m["hb", level][...], axis=0)
+        z = (local + outer(hq, exp[level][...])) * piv[level][...]
+        saved[level] = z
+        m["za", level][near] = mult(z, exp[level][...])
+        spread_own(("za", level), NEAR, 1)
+
+    def pass_zp(level):
+        m["zb", level][far % nb[level]] = near_sum(("za", level))
+        spread_own(("zb", level), nb[level], NEAR)
+
+    def base_of(level, zp):
+        return outer(saved[level], blk[level][...]) + outer(zp * head[level], q_of(level))
+
+    def tail_of(level, wv):
+        qm = q_of(level) * jnp.broadcast_to(head[level][:1], (LANES, RANK))
+        keep(("t", level), wv + times(qm, kept(("cross", level)), 0))
+
+    def wv_of(level):
+        qh, ql = kept(("qw", level))
+        return qh[:, RANK:].astype(F32) + ql[:, RANK:].astype(F32)
+
+    arrive("r0")
+    r0 = m["r0"][...]
+    lane = lax.broadcasted_iota(jnp.int32, (plane, 2 * LANES), 1).astype(F32)
+    at = cap * count
+    m["oh0"][...] = jnp.concatenate(
+        [(lane == r0[:, at + s : at + s + 1]).astype(F32) for s in range(cap)], axis=1
+    ).astype(BF16)
+    inc = spread(r0, m["oh0"][...], cap, count)
+    b1 = src[1][...] + inc[:, :LANES]
+    send_up(1, b1, inc[:, LANES:])
+
+    local1 = mult(b1, blk[1][...])
+    saved[0] = z0
+    arrive("zx")
+    base0 = base_of(0, jnp.sum(m["zx"][...], axis=0))
+    build(1)
+    arrive("xg1")
+    keep(("cross", 1), m["xg1"][...].reshape(RANK, RANK))
+    build(2)
+    kh, kl = kept(("qw", 3))
+    hot, gh, gl = m["ohg", 2][...], *kept(("g", 2))
+    m["kp"][...] = (once(hot, kh, 1, 0) + once(hot, kl, 1, 0)).reshape(NEAR, fars, 2 * RANK)
+    scatter_near("kr", "kp")
+    arrive("xb2")
+    m["xy"][me // plane] = jnp.sum(m["xb2"][...], axis=0)
+    spread_own("xy", total_devices // plane, plane)
+    send_on(1)
+    both = once(gh, kh, 1, 0) + (once(gl, kh, 1, 0) + once(gh, kl, 1, 0))
+    m["yp"][...] = both.reshape(NEAR, 2 * RANK // NEAR, 2 * RANK)
+    scatter_near("yr", "yp")
+
+    arrive("xy")
+    pair = me // plane // 2 * 2
+    m["xg2"][near, :slice_rows, :] = jnp.sum(m["xy"][pl.ds(pair, 2), :slice_rows, :], axis=0)
+    m["xg2"][near, slice_rows:, :] = jnp.sum(m["xy"][:, slice_rows:, :], axis=0)
+    spread_own("xg2", NEAR, 1)
+    tail_of(1, wv_of(1))
+
+    inc = receive_up(1)
+    b2 = src[2][...] + inc[:, :LANES]
+    send_up(2, b2, inc[:, LANES:])
+
+    local2 = mult(b2, blk[2][...])
+    arrive("xg2")
+    keep(("cross", 2), m["xg2"][:, :slice_rows, :].reshape(RANK, RANK))
+    send_on(2)
+    m["yg"][near] = near_sum("yr")
+    spread_own("yg", NEAR, 1)
+    keep(("cross", 3), m["xg2"][:, slice_rows:, :].reshape(RANK, RANK))
+    root_qm = q_of(3) * jnp.broadcast_to(head[3][:1], (LANES, RANK))
+    root_t = wv_of(3) + times(root_qm, kept(("cross", 3)), 0)
+    keep(("qt", 3), jnp.concatenate([root_qm, root_t], axis=1))
+    solve_front(1, local1)
+    tail_of(2, wv_of(2))
+
+    b3 = src[3][...] + receive_up(2)
+    both = times(b3, kept(("qt", 3)), 0)
+    core = near // across
+    m["fs3"][0] = both[:, :RANK]
+    m["fs3"][1] = both[:, RANK:]
+    m["fa", 3][near] = m["fs3"][core]
+    fan_near(("fa", 3), lambda q: m["fs3"].at[q // across], m["fa", 3])
+    early = outer(mult(b3, blk[3][...]) * piv[3][...], blk[3][...])
+    send_down(2, early)
+    solve_front(2, local2)
+    pass_zp(1)
+    m["fb"][far] = near_sum(("fa", 3))
+    spread_own("fb", fars, NEAR)
+    arrive("c0")
+    keep(("cross", 0), jnp.sum(m["c0"][...], axis=0))
+    tail_of(0, mult(blk[0][...], v_of(0)))
+    arrive(("ba", 2))
+    ba = m["ba", 2]
+    sums = jnp.sum(ba[:, : 2 * count, :], axis=0)
+    early_rows = rows_of(2, "s", ba[:, 2 * count :, :])
+    pass_zp(2)
+    arrive("yg")
+    arrive("kr")
+    keep("ka", m["kr"][...].reshape(NEAR * fars, 2 * RANK))
+    keep("y", m["yg"][...].reshape(2 * RANK, 2 * RANK))
+    arrive(("zb", 1))
+    base1 = base_of(1, jnp.sum(m["zb", 1][...], axis=0))
+    arrive("fb")
+    m["fc"][core] = jnp.sum(m["fb"][...], axis=0)
+    spread_own("fc", 2, across)
+    arrive("fc")
+    ends = jnp.concatenate([m["fc"][1] * head[3], m["fc"][0]], axis=1)
+    sums = jnp.concatenate([sums[:count], sums[count:]], axis=1) + times(ends, kept("y"), 1)
+    late = times(ends, kept("ka"), 1)
+    per = LANES // fars
+    late = [
+        pltpu.roll(late[:, k // per * LANES : (k // per + 1) * LANES], (LANES - k % per * fars) % LANES, 1)
+        for k in range(NEAR)
+    ]
+    late = transposed(jnp.concatenate(late, axis=0))[:fars]
+    send_far(2, "s", sums[:, :RANK], sums[:, RANK:], early_rows + late)
+    spread_own("hx", four, 1)
+    outs[3][...] = early + times(ends, kept(("qw", 3)), 1)
+
     arrive(("zb", 2))
     base2 = base_of(2, jnp.sum(m["zb", 2][...], axis=0))
-    send_further(2)
     x, xu = receive_down(2, base2)
     send_down(1, jnp.concatenate([x, xu], axis=1))
     outs[2][...] = x
     send_further(1)
+    arrive("hx")
+    for k in range(four):
+        at = slice(k * cap * plane, (k + 1) * cap * plane)
+        m["hxh"][at, :], m["hxl"][at, :] = halves(m["hx"][k])
     x, xu = receive_down(1, base1)
     full = diagonal(jnp.concatenate([x, xu], axis=1), cap, four)
     rows = leaf_rows((m["oh0"][...], None), full)
@@ -706,6 +736,11 @@
             "oh0": bits(size[1], cap * 2 * LANES),
             "fb": vm(nb[3], count, LANES),
             "fs3": vm(2, count, LANES),
+            "kp": vm(NEAR, nb[3], 2 * RANK),
+            "kr": vm(NEAR, nb[3], 2 * RANK),
+            "yp": vm(NEAR, 2 * RANK // NEAR, 2 * RANK),
+            "yr": vm(NEAR, 2 * RANK // NEAR, 2 * RANK),
+            "yg": vm(NEAR, 2 * RANK // NEAR, 2 * RANK),
             "fc": vm(2, count, LANES),
             "hx": vm(size[0], cap * size[1], RANK),
             "hxh": bits(size[0] * cap * size[1], RANK),
@@ -713,6 +748,9 @@
         }
         for name in ("s0", "r0", "s0b", "r0b"):
             bufs[name] = vm(size[1], LANES)
+        for half in "hl":
+            bufs["ka", half] = bits(NEAR * nb[3], 2 * RANK)
+            bufs["y", half] = bits(2 * RANK, 2 * RANK)
         for i in range(4):
             for half in "hl":
                 bufs[("cross", i), half] = bits(RANK, RANK)
@@ -745,28 +783,27 @@
             bufs["hb", i] = vm(nb[i], count, LANES)
             bufs["za", i] = vm(NEAR, count, LANES)
             bufs["zb", i] = vm(nb[i], count, LANES)
-        arrays = [*src, *blk, *exp, *bas, *piv, *cl, *tgt]
+        arrays = [*src, *blk, *exp, *bas, *piv, *cl, *tgt, *rnk]
         for i, v in enumerate(arrays):
             bufs["in", i] = pltpu.VMEM(v.shape, v.dtype)
         scratch = list(bufs.values())
         scratch += [
             pltpu.SemaphoreType.DMA((48,)),
             pltpu.SemaphoreType.DMA((48,)),
-            pltpu.SemaphoreType.DMA((26,)),
+            pltpu.SemaphoreType.DMA((30,)),
             pltpu.SemaphoreType.REGULAR,
         ]
         vspec = pl.BlockSpec(memory_space=pltpu.VMEM)
-        sspec = pl.BlockSpec(memory_space=pltpu.SMEM)
         whole = pl.pallas_call(
             functools.partial(kernel, (leaves, across, size, ups, count, cap), list(bufs)),
             out_shape=jax.ShapeDtypeStruct((4 * count, LANES), F32),
-            in_specs=[pl.BlockSpec(memory_space=pl.ANY)] * 26 + [sspec] * 4,
+            in_specs=[pl.BlockSpec(memory_space=pl.ANY)] * 30,
             out_specs=vspec,
             scratch_shapes=scratch,
             compiler_params=pltpu.CompilerParams(
                 collective_id=0, has_side_effects=True, vmem_limit_bytes=60 * 1024 * 1024
             ),
-        )(*arrays, *rnk)
+        )(*arrays)
         return tuple(whole[i * count : (i + 1) * count] for i in range(4))
 
     spread_axes = ("leaf", "grid")

time: 88.8 us -> 84.5 us (0.952)
  Pallas kernels: 86.7 us -> 82.3 us
    pallas_call x1, Pallas kernels: 86.7 us -> 82.3 us  [shards(): pl.pallas_call(functools.partial(kernel, (leaves, across, size, ups, coun...]
where the time goes in v4:
time: 84.5 us; the launch traced here: 84.3 us
  Pallas kernels  82.3 us (97%)
  local copies, waits for them, and re-layouts  1.3 us (2%)
    pallas_call x1, Pallas kernels, shards(): pl.pallas_call(functools.partial(kernel, (leaves, across, size, ups, coun...  82.3 us

profile of v4, /device:TPU:1, one launch (start us, length us, event | category | flops | bytes accessed | tf_op | source)
XLA Modules:
  0.0 84.3 jit_solution(9223245923190200537)
XLA Ops:
  0.6 82.3 %shard_map.309 = f32[32,128]{1,0:T(8,128)} custom-call(f32[8,128]{1,0:T(8,128)} %refs_0_.1, f32[8,128]{1,0:T(8,128)} %refs_1_.1, f32[8,128]{1,0:T(8,128)} %refs_2_.1, f32[8,128]{1,0:T(8,128)} %refs_3_.1, f32[128,128]{1,0:T(8,128)} %refs_4_.1, f32[128,128]{1,0:T(8,128)} %refs_5_.1, f32[128,128]{1,0:T(8,128)} %refs_6_.1, f32[128,128]{1,0:T(8,128)} %refs_7_.1, ...), custom_call_target="tpu_custom_call" | custom-call | tf_op jit(solution)/shard_map/pallas_call | solution.py:797
  83.0 1.3 %fusion = (f32[8,128]{1,0:T(8,128)}, f32[8,128]{1,0:T(8,128)}, f32[8,128]{1,0:T(8,128)}, f32[8,128]{1,0:T(8,128)}) fusion(f32[32,128]{1,0:T(8,128)} %shard_map.309), kind=kLoop, calls=%fused_computation | loop fusion | bytes 32768 | tf_op jit(solution)/shard_map/slice | solution.py:807

commit v5 on v4

--- a/solution.py
+++ b/solution.py
@@ -482,21 +482,25 @@
         tot = jnp.sum(fa[:, : 2 * count, :], axis=0)
         hq = tot[:count] * head[level]
         w = tot[count:] + times(hq, kept(("cross", level)), 0)
-        send_far(level, "w", w, w, rows_of(level, "w", fa[:, 2 * count :, :]))
+        rows = rows_of(level, "w", fa[:, 2 * count :, :])
+        send_far(level, "w", w, w, rows)
         m["hb", level][far % nb[level]] = hq
         spread_own(("hb", level), nb[level], NEAR)
-
-    def receive_up(level):
-        n = nb[level + 1]
-        half = n // 2
+        return rows
+
+    def sums_up(level):
+        half = nb[level + 1] // 2
         arrive(("w", level))
         wb = m["wb", level]
-        ws = []
-        for child in range(2):
-            mc = below[level][child]
-            ws.append(jnp.sum(wb[child * half : (child + 1) * half, :count, :], axis=0) * mc)
-        inc = -times(jnp.concatenate(ws, axis=1), kept(("g", level)), 0)
-        return inc + spread(wb[:, count, :], m["ohf", level][...], NEAR, count)
+        ws = [
+            jnp.sum(wb[child * half : (child + 1) * half, :count, :], axis=0) * below[level][child]
+            for child in range(2)
+        ]
+        return jnp.concatenate(ws, axis=1)
+
+    def receive_up(level, ws):
+        rows = spread(m["wb", level][:, count, :], m["ohf", level][...], NEAR, count)
+        return rows - times(ws, kept(("g", level)), 0)
 
     def near_sum(name):
         arrive(name)
@@ -583,6 +587,20 @@
     both = once(gh, kh, 1, 0) + (once(gl, kh, 1, 0) + once(gh, kl, 1, 0))
     m["yp"][...] = both.reshape(NEAR, 2 * RANK // NEAR, 2 * RANK)
     scatter_near("yr", "yp")
+    ks, kb = m["ks"], m["kb"]
+    for half in range(2):
+        ks[:, half] = m["kp"][:, :, half * RANK : (half + 1) * RANK]
+    kb[:, :, pl.ds(far, 1), :] = ks[:, :, pl.ds(far, 1), :]
+    fan(
+        fars,
+        NEAR,
+        (
+            "kb",
+            lambda q: ks.at[:, :, pl.ds(q, 1)],
+            lambda i: kb.at[:, :, pl.ds(i, 1)],
+            kb.at[:, :, pl.ds(0, fars - 1)],
+        ),
+    )
 
     arrive("xy")
     pair = me // plane // 2 * 2
@@ -591,36 +609,50 @@
     spread_own("xg2", NEAR, 1)
     tail_of(1, wv_of(1))
 
-    inc = receive_up(1)
+    inc = receive_up(1, sums_up(1))
     b2 = src[2][...] + inc[:, :LANES]
     send_up(2, b2, inc[:, LANES:])
+    m["yg"][near] = near_sum("yr")
+    spread_own("yg", NEAR, 1)
 
     local2 = mult(b2, blk[2][...])
     arrive("xg2")
     keep(("cross", 2), m["xg2"][:, :slice_rows, :].reshape(RANK, RANK))
-    send_on(2)
-    m["yg"][near] = near_sum("yr")
-    spread_own("yg", NEAR, 1)
+    rows = send_on(2)
     keep(("cross", 3), m["xg2"][:, slice_rows:, :].reshape(RANK, RANK))
-    root_qm = q_of(3) * jnp.broadcast_to(head[3][:1], (LANES, RANK))
-    root_t = wv_of(3) + times(root_qm, kept(("cross", 3)), 0)
-    keep(("qt", 3), jnp.concatenate([root_qm, root_t], axis=1))
+    core = near // across
+    per = LANES // fars
+    turned = transposed(rows)
+    passing = []
+    for t in range(NEAR // per):
+        group = [turned[(t * per + k) * count : (t * per + k + 1) * count] for k in range(per)]
+        passing.append(sum(pltpu.roll(group[k], k * fars, 1) for k in range(1, per)) + group[0])
+    arrive("kb")
+    pulled = jnp.concatenate([kb[:, half].reshape(NEAR * fars, RANK) for half in range(2)], axis=1)
+    sr = times(src[3][...], kept(("qw", 3)), 0)
+    sr = sr + times(jnp.concatenate(passing, axis=1), halves(pulled), 0)
+    m["sr"][near] = jnp.concatenate([sr[:, :RANK], sr[:, RANK:]], axis=0)
+    spread_own("sr", NEAR, 1)
     solve_front(1, local1)
     tail_of(2, wv_of(2))
 
-    b3 = src[3][...] + receive_up(2)
-    both = times(b3, kept(("qt", 3)), 0)
-    core = near // across
-    m["fs3"][0] = both[:, :RANK]
-    m["fs3"][1] = both[:, RANK:]
-    m["fa", 3][near] = m["fs3"][core]
-    fan_near(("fa", 3), lambda q: m["fs3"].at[q // across], m["fa", 3])
+    arrive("yg")
+    y = m["yg"][...].reshape(2 * RANK, 2 * RANK)
+    keep("y", y)
+    yq = y[:, :RANK] * jnp.broadcast_to(head[3][:1], (2 * RANK, RANK))
+    yv = y[:, RANK:] + times(yq, kept(("cross", 3)), 0)
+    keep("yh", jnp.where(core == 0, yq, yv))
+    tot = near_sum("sr")
+    sq = tot[:count] * head[3]
+    mine = jnp.where(core == 0, sq, tot[count:] + times(sq, kept(("cross", 3)), 0))
+    ws = sums_up(2)
+    m["fb"][far] = mine - times(ws, kept("yh"), 0)
+    spread_own("fb", fars, NEAR)
+    b3 = src[3][...] + receive_up(2, ws)
     early = outer(mult(b3, blk[3][...]) * piv[3][...], blk[3][...])
     send_down(2, early)
     solve_front(2, local2)
     pass_zp(1)
-    m["fb"][far] = near_sum(("fa", 3))
-    spread_own("fb", fars, NEAR)
     arrive("c0")
     keep(("cross", 0), jnp.sum(m["c0"][...], axis=0))
     tail_of(0, mult(blk[0][...], v_of(0)))
@@ -629,10 +661,8 @@
     sums = jnp.sum(ba[:, : 2 * count, :], axis=0)
     early_rows = rows_of(2, "s", ba[:, 2 * count :, :])
     pass_zp(2)
-    arrive("yg")
     arrive("kr")
     keep("ka", m["kr"][...].reshape(NEAR * fars, 2 * RANK))
-    keep("y", m["yg"][...].reshape(2 * RANK, 2 * RANK))
     arrive(("zb", 1))
     base1 = base_of(1, jnp.sum(m["zb", 1][...], axis=0))
     arrive("fb")
@@ -642,7 +672,6 @@
     ends = jnp.concatenate([m["fc"][1] * head[3], m["fc"][0]], axis=1)
     sums = jnp.concatenate([sums[:count], sums[count:]], axis=1) + times(ends, kept("y"), 1)
     late = times(ends, kept("ka"), 1)
-    per = LANES // fars
     late = [
         pltpu.roll(late[:, k // per * LANES : (k // per + 1) * LANES], (LANES - k % per * fars) % LANES, 1)
         for k in range(NEAR)
@@ -735,7 +764,9 @@
             "low0": vm(size[1], LANES),
             "oh0": bits(size[1], cap * 2 * LANES),
             "fb": vm(nb[3], count, LANES),
-            "fs3": vm(2, count, LANES),
+            "ks": vm(NEAR, 2, nb[3], RANK),
+            "kb": vm(NEAR, 2, nb[3], RANK),
+            "sr": vm(NEAR, 2 * count, LANES),
             "kp": vm(NEAR, nb[3], 2 * RANK),
             "kr": vm(NEAR, nb[3], 2 * RANK),
             "yp": vm(NEAR, 2 * RANK // NEAR, 2 * RANK),
@@ -751,13 +782,12 @@
         for half in "hl":
             bufs["ka", half] = bits(NEAR * nb[3], 2 * RANK)
             bufs["y", half] = bits(2 * RANK, 2 * RANK)
+            bufs["yh", half] = bits(2 * RANK, RANK)
         for i in range(4):
             for half in "hl":
                 bufs[("cross", i), half] = bits(RANK, RANK)
                 bufs[("qw", i), half] = bits(LANES, 2 * RANK)
                 bufs[("t", i), half] = bits(LANES, RANK)
-                bufs[("qt", i), half] = bits(LANES, 2 * RANK)
-        bufs["fa", 3] = vm(NEAR, count, LANES)
         for i in (1, 2):
             n = nb[i + 1]
             wide = 2 * LANES if i == 1 else LANES
@@ -788,8 +818,8 @@
             bufs["in", i] = pltpu.VMEM(v.shape, v.dtype)
         scratch = list(bufs.values())
         scratch += [
-            pltpu.SemaphoreType.DMA((48,)),
-            pltpu.SemaphoreType.DMA((48,)),
+            pltpu.SemaphoreType.DMA((56,)),
+            pltpu.SemaphoreType.DMA((56,)),
             pltpu.SemaphoreType.DMA((30,)),
             pltpu.SemaphoreType.REGULAR,
         ]

time: 84.5 us -> 81.6 us (0.966)
  Pallas kernels: 82.3 us -> 79.4 us
    pallas_call x1, Pallas kernels: 82.3 us -> 79.4 us  [shards(): pl.pallas_call(functools.partial(kernel, (leaves, across, size, ups, coun...]
where the time goes in v5:
time: 81.6 us; the launch traced here: 81.4 us
  Pallas kernels  79.4 us (97%)
  local copies, waits for them, and re-layouts  1.3 us (2%)
    pallas_call x1, Pallas kernels, shards(): pl.pallas_call(functools.partial(kernel, (leaves, across, size, ups, coun...  79.4 us

profile of v5, /device:TPU:1, one launch (start us, length us, event | category | flops | bytes accessed | tf_op | source)
XLA Modules:
  0.0 81.4 jit_solution(4437554615967810661)
XLA Ops:
  0.6 79.4 %shard_map.309 = f32[32,128]{1,0:T(8,128)} custom-call(f32[8,128]{1,0:T(8,128)} %refs_0_.1, f32[8,128]{1,0:T(8,128)} %refs_1_.1, f32[8,128]{1,0:T(8,128)} %refs_2_.1, f32[8,128]{1,0:T(8,128)} %refs_3_.1, f32[128,128]{1,0:T(8,128)} %refs_4_.1, f32[128,128]{1,0:T(8,128)} %refs_5_.1, f32[128,128]{1,0:T(8,128)} %refs_6_.1, f32[128,128]{1,0:T(8,128)} %refs_7_.1, ...), custom_call_target="tpu_custom_call" | custom-call | tf_op jit(solution)/shard_map/pallas_call | solution.py:827
  80.1 1.3 %fusion = (f32[8,128]{1,0:T(8,128)}, f32[8,128]{1,0:T(8,128)}, f32[8,128]{1,0:T(8,128)}, f32[8,128]{1,0:T(8,128)}) fusion(f32[32,128]{1,0:T(8,128)} %shard_map.309), kind=kLoop, calls=%fused_computation | loop fusion | bytes 32768 | tf_op jit(solution)/shard_map/slice | solution.py:837

commit v6 on v5

--- a/solution.py
+++ b/solution.py
@@ -184,16 +184,24 @@
 
         lax.fori_loop(1, NEAR, body, 0)
 
-    def greet_far(k, carry):
-        peer = (far + k) % fars * NEAR + near
-        pl.semaphore_signal(barrier, inc=1, device_id=peer, device_id_type=LOGICAL)
-        return carry
-
-    lax.fori_loop(1, fars, greet_far, 0)
+    def greet_ring(sem):
+        for dz in farthest(ring)[:-1]:
+            peer = (far // ring * ring + (far + dz) % ring) * NEAR + near
+            pl.semaphore_signal(sem, inc=1, device_id=peer, device_id_type=LOGICAL)
+
+    def greet_planes():
+        for dy in range(1, fars // ring):
+            peer = (far + dy * ring) % fars * NEAR + near
+            pl.semaphore_signal(barrier, inc=1, device_id=peer, device_id_type=LOGICAL)
+
+    soon = (0, 12)
+    for i in soon:
+        loads[i].start()
+    greet_ring(barrier)
+    greet_planes()
     greet_near(barrier)
-    soon = (0, 12)
     rest = [i for i in range(count_in) if i not in soon]
-    for i in soon + tuple(rest):
+    for i in rest:
         loads[i].start()
 
     def mask(level, which, front):
@@ -215,15 +223,24 @@
         n = nb[level + 1]
         return NEAR * n // LANES, LANES // n
 
+    def keep(name, value):
+        hi, lo = halves(value)
+        m[name, "h"][...] = hi
+        m[name, "l"][...] = lo
+
+    def kept(name):
+        return m[name, "h"][...], m[name, "l"][...]
+
     four = size[0]
     my4 = me % four
     for i in soon:
         loads[i].wait()
     s0 = src[0][...]
     m["f1"][my4] = mult(s0, q_of(0))
-    pl.semaphore_wait(barrier, NEAR - 1 + fars - 1)
+    pl.semaphore_wait(barrier, NEAR - 1 + ring - 1 + fars // ring - 1)
+    spread_own("f1", four, 1)
     greet_near(ready)
-    spread_own("f1", four, 1)
+    greet_ring(ready)
     for i in rest:
         loads[i].wait()
     front = [me // n for n in size]
@@ -233,7 +250,10 @@
         [mask(level, 1, front[level + 1] * 2 + child) for child in range(2)] for level in (1, 2)
     ]
     local0 = mult(s0, blk[0][...])
-    m["c0"][my4] = inner(exp[0][...], v_of(0))
+    own0 = inner(exp[0][...], v_of(0))
+    m["c0"][my4] = own0
+    keep("own", own0)
+    lv0 = mult(local0, v_of(0))
 
     slice_rows = RANK // NEAR
     root_piv = jnp.broadcast_to(piv[3][...], (LANES, LANES)).T
@@ -315,14 +335,6 @@
     fan_near("la", lambda q: m["lows"].at[q // 4], m["la"])
     scatter_near(("ra", 1), ("pa", 1))
 
-    def keep(name, value):
-        hi, lo = halves(value)
-        m[name, "h"][...] = hi
-        m[name, "l"][...] = lo
-
-    def kept(name):
-        return m[name, "h"][...], m[name, "l"][...]
-
     for level in (1, 2):
         wv = mult(blk[level][...], v_of(level))
         keep(("qw", level), jnp.concatenate([q_of(level), wv], axis=1))
@@ -331,9 +343,9 @@
 
     arrive("f1")
     hq0 = jnp.sum(m["f1"][...], axis=0) * head[0]
+    m["fv"][my4] = lv0 + times(hq0, kept("own"), 0)
+    spread_own("fv", four, 1)
     y0 = local0 + outer(hq0, exp[0][...])
-    m["fv"][my4] = mult(y0, v_of(0))
-    spread_own("fv", four, 1)
     scatter_near(("ra", 2), ("pa", 2))
     scatter_near("xr2", "xp2")
     z0 = y0 * piv[0][...]
@@ -367,7 +379,7 @@
 
     hc = (m["hch"][...], m["hcl"][...])
     m["s0"][...] = leaf_rows(hc, diagonal(-w0, cap)) + m["low0"][...]
-    pl.semaphore_wait(ready, NEAR - 1)
+    pl.semaphore_wait(ready, NEAR - 1 + ring - 1)
     send_leaf("s0", "r0", lambda q: q)
 
     def store_row(buf, i, row):
@@ -405,7 +417,10 @@
     m["tl"][...] = transposed(m["la"][...].reshape(NEAR * count, LANES))
     for level in (1, 2):
         arrive(("ra", level))
-        fan(nb[level + 1], NEAR, forward_rows(level, "tl", ("lb", level), ("lb", level)), couple_set(level))
+        sets = [forward_rows(level, "tl", ("lb", level), ("lb", level))]
+        if level == 1:
+            sets.append(couple_set(level))
+        fan(nb[level + 1], NEAR, *sets)
     arrive("xr2")
     m["xb2"][far % ring] = jnp.sum(m["xr2"][...], axis=0)
     spread_own("xb2", ring, NEAR)
@@ -413,9 +428,8 @@
     m["xg1"][near] = jnp.sum(m["xb1"][...], axis=0)
     spread_own("xg1", NEAR, 1)
     spread_own("zx", four, 1)
-    spread_own("c0", four, 1)
-
-    def build(level):
+
+    def build_hits(level):
         n = nb[level + 1]
         wide = 2 * LANES if level == 1 else LANES
         arrive(("lb", level))
@@ -425,6 +439,10 @@
         hits = [(lane == lb[:, k * count + at : k * count + at + 1]).astype(F32) for k in range(NEAR)]
         m["ohf", level][...] = jnp.concatenate(hits, axis=1).astype(BF16)
         m["ohg", level][...] = jnp.concatenate(hits, axis=0).astype(BF16)
+        return hits
+
+    def build_g(level, hits):
+        n = nb[level + 1]
         arrive(("rb", level))
         half = n // 2
         for child in range(2):
@@ -567,26 +585,24 @@
     inc = spread(r0, m["oh0"][...], cap, count)
     b1 = src[1][...] + inc[:, :LANES]
     send_up(1, b1, inc[:, LANES:])
+    fan(nb[3], NEAR, couple_set(2))
 
     local1 = mult(b1, blk[1][...])
     saved[0] = z0
     arrive("zx")
     base0 = base_of(0, jnp.sum(m["zx"][...], axis=0))
-    build(1)
+    build_g(1, build_hits(1))
     arrive("xg1")
     keep(("cross", 1), m["xg1"][...].reshape(RANK, RANK))
-    build(2)
+    hits = build_hits(2)
     kh, kl = kept(("qw", 3))
-    hot, gh, gl = m["ohg", 2][...], *kept(("g", 2))
+    hot = m["ohg", 2][...]
     m["kp"][...] = (once(hot, kh, 1, 0) + once(hot, kl, 1, 0)).reshape(NEAR, fars, 2 * RANK)
     scatter_near("kr", "kp")
     arrive("xb2")
     m["xy"][me // plane] = jnp.sum(m["xb2"][...], axis=0)
     spread_own("xy", total_devices // plane, plane)
     send_on(1)
-    both = once(gh, kh, 1, 0) + (once(gl, kh, 1, 0) + once(gh, kl, 1, 0))
-    m["yp"][...] = both.reshape(NEAR, 2 * RANK // NEAR, 2 * RANK)
-    scatter_near("yr", "yp")
     ks, kb = m["ks"], m["kb"]
     for half in range(2):
         ks[:, half] = m["kp"][:, :, half * RANK : (half + 1) * RANK]
@@ -607,6 +623,11 @@
     m["xg2"][near, :slice_rows, :] = jnp.sum(m["xy"][pl.ds(pair, 2), :slice_rows, :], axis=0)
     m["xg2"][near, slice_rows:, :] = jnp.sum(m["xy"][:, slice_rows:, :], axis=0)
     spread_own("xg2", NEAR, 1)
+    build_g(2, hits)
+    gh, gl = kept(("g", 2))
+    both = once(gh, kh, 1, 0) + (once(gl, kh, 1, 0) + once(gh, kl, 1, 0))
+    m["yp"][...] = both.reshape(NEAR, 2 * RANK // NEAR, 2 * RANK)
+    scatter_near("yr", "yp")
     tail_of(1, wv_of(1))
 
     inc = receive_up(1, sums_up(1))
@@ -633,6 +654,7 @@
     sr = sr + times(jnp.concatenate(passing, axis=1), halves(pulled), 0)
     m["sr"][near] = jnp.concatenate([sr[:, :RANK], sr[:, RANK:]], axis=0)
     spread_own("sr", NEAR, 1)
+    spread_own("c0", four, 1)
     solve_front(1, local1)
     tail_of(2, wv_of(2))
 
@@ -663,8 +685,6 @@
     pass_zp(2)
     arrive("kr")
     keep("ka", m["kr"][...].reshape(NEAR * fars, 2 * RANK))
-    arrive(("zb", 1))
-    base1 = base_of(1, jnp.sum(m["zb", 1][...], axis=0))
     arrive("fb")
     m["fc"][core] = jnp.sum(m["fb"][...], axis=0)
     spread_own("fc", 2, across)
@@ -681,6 +701,8 @@
     spread_own("hx", four, 1)
     outs[3][...] = early + times(ends, kept(("qw", 3)), 1)
 
+    arrive(("zb", 1))
+    base1 = base_of(1, jnp.sum(m["zb", 1][...], axis=0))
     arrive(("zb", 2))
     base2 = base_of(2, jnp.sum(m["zb", 2][...], axis=0))
     x, xu = receive_down(2, base2)
@@ -690,7 +712,8 @@
     arrive("hx")
     for k in range(four):
         at = slice(k * cap * plane, (k + 1) * cap * plane)
-        m["hxh"][at, :], m["hxl"][at, :] = halves(m["hx"][k])
+        packed = m["hx"][k] * jnp.broadcast_to(side[0][:1], (cap * plane, RANK))
+        m["hxh"][at, :], m["hxl"][at, :] = halves(times(packed, kept(("t", 0)), 1))
     x, xu = receive_down(1, base1)
     full = diagonal(jnp.concatenate([x, xu], axis=1), cap, four)
     rows = leaf_rows((m["oh0"][...], None), full)
@@ -701,15 +724,13 @@
     m["s0b"][...] = rows + pltpu.roll(rows, plane - 2, 0)
     send_leaf("s0b", "r0b", lambda q: q // four * four)
     outs[1][...] = x
+    for name, part in parts.items():
+        wait_for(part, send_sem.at[sem_of(name)])
     arrive("r0b")
     rows = transposed(m["r0b"][...])
     pieces = [rows[g * count : (g + 1) * count] for g in range(four * cap)]
     pairs = [pieces[2 * g] + pltpu.roll(pieces[2 * g + 1], plane, 1) for g in range(four * cap // 2)]
-    s = times(jnp.concatenate(pairs, axis=1), (m["hxh"][...], m["hxl"][...]), 0) * side[0]
-    outs[0][...] = base0 - times(s, kept(("t", 0)), 1)
-
-    for name, part in parts.items():
-        wait_for(part, send_sem.at[sem_of(name)])
+    outs[0][...] = base0 - times(jnp.concatenate(pairs, axis=1), (m["hxh"][...], m["hxl"][...]), 0)
 
 
 def solution(mesh):
@@ -788,6 +809,7 @@
                 bufs[("cross", i), half] = bits(RANK, RANK)
                 bufs[("qw", i), half] = bits(LANES, 2 * RANK)
                 bufs[("t", i), half] = bits(LANES, RANK)
+                bufs["own", half] = bits(RANK, RANK)
         for i in (1, 2):
             n = nb[i + 1]
             wide = 2 * LANES if i == 1 else LANES

time: 81.6 us -> 79.1 us (0.969)
  Pallas kernels: 79.4 us -> 77 us
    pallas_call x1, Pallas kernels: 79.4 us -> 77 us  [shards(): pl.pallas_call(functools.partial(kernel, (leaves, across, size, ups, coun...]
where the time goes in v6:
time: 79.1 us; the launch traced here: 79 us
  Pallas kernels  77 us (97%)
  local copies, waits for them, and re-layouts  1.3 us (2%)
    pallas_call x1, Pallas kernels, shards(): pl.pallas_call(functools.partial(kernel, (leaves, across, size, ups, coun...  77 us

profile of v6, /device:TPU:1, one launch (start us, length us, event | category | flops | bytes accessed | tf_op | source)
XLA Modules:
  0.0 79.0 jit_solution(18112388174553846939)
XLA Ops:
  0.6 77.0 %shard_map.309 = f32[32,128]{1,0:T(8,128)} custom-call(f32[8,128]{1,0:T(8,128)} %refs_0_.1, f32[8,128]{1,0:T(8,128)} %refs_1_.1, f32[8,128]{1,0:T(8,128)} %refs_2_.1, f32[8,128]{1,0:T(8,128)} %refs_3_.1, f32[128,128]{1,0:T(8,128)} %refs_4_.1, f32[128,128]{1,0:T(8,128)} %refs_5_.1, f32[128,128]{1,0:T(8,128)} %refs_6_.1, f32[128,128]{1,0:T(8,128)} %refs_7_.1, ...), custom_call_target="tpu_custom_call" | custom-call | tf_op jit(solution)/shard_map/pallas_call | solution.py:849
  77.7 1.3 %fusion = (f32[8,128]{1,0:T(8,128)}, f32[8,128]{1,0:T(8,128)}, f32[8,128]{1,0:T(8,128)}, f32[8,128]{1,0:T(8,128)}) fusion(f32[32,128]{1,0:T(8,128)} %shard_map.309), kind=kLoop, calls=%fused_computation | loop fusion | bytes 32768 | tf_op jit(solution)/shard_map/slice | solution.py:859

commit v7 on v6

--- a/solution.py
+++ b/solution.py
@@ -189,16 +189,21 @@
             peer = (far // ring * ring + (far + dz) % ring) * NEAR + near
             pl.semaphore_signal(sem, inc=1, device_id=peer, device_id_type=LOGICAL)
 
-    def greet_planes():
-        for dy in range(1, fars // ring):
+    def greet_z(sem, step):
+        for dz in (step, ring - step):
+            peer = (far // ring * ring + (far + dz) % ring) * NEAR + near
+            pl.semaphore_signal(sem, inc=1, device_id=peer, device_id_type=LOGICAL)
+
+    def greet_y(sem):
+        for dy in (1, fars // ring - 1):
             peer = (far + dy * ring) % fars * NEAR + near
-            pl.semaphore_signal(barrier, inc=1, device_id=peer, device_id_type=LOGICAL)
+            pl.semaphore_signal(sem, inc=1, device_id=peer, device_id_type=LOGICAL)
 
     soon = (0, 12)
     for i in soon:
         loads[i].start()
-    greet_ring(barrier)
-    greet_planes()
+    greet_z(barrier, 1)
+    greet_y(barrier)
     greet_near(barrier)
     rest = [i for i in range(count_in) if i not in soon]
     for i in rest:
@@ -237,10 +242,10 @@
         loads[i].wait()
     s0 = src[0][...]
     m["f1"][my4] = mult(s0, q_of(0))
-    pl.semaphore_wait(barrier, NEAR - 1 + ring - 1 + fars // ring - 1)
+    pl.semaphore_wait(barrier, NEAR - 1 + 4)
     spread_own("f1", four, 1)
-    greet_near(ready)
-    greet_ring(ready)
+    greet_z(ready.at[0], 1)
+    greet_y(ready.at[0])
     for i in rest:
         loads[i].wait()
     front = [me // n for n in size]
@@ -330,6 +335,8 @@
         m[name][near] = m[source][near]
         fan_near(name, lambda q: m[source].at[q], m[name])
 
+    pl.semaphore_wait(ready.at[0], 4)
+    greet_z(ready.at[1], 2)
     scatter_near("xr1", "xp1")
     m["la"][near] = m["lows"][near // 4]
     fan_near("la", lambda q: m["lows"].at[q // 4], m["la"])
@@ -341,6 +348,9 @@
     wpp = mult(blk[3][...] * piv[3][...], exp[3][...])
     keep(("qw", 3), jnp.concatenate([q_of(3), wpp], axis=1))
 
+    pl.semaphore_wait(ready.at[1], 2)
+    greet_near(ready.at[2])
+    greet_ring(ready.at[2])
     arrive("f1")
     hq0 = jnp.sum(m["f1"][...], axis=0) * head[0]
     m["fv"][my4] = lv0 + times(hq0, kept("own"), 0)
@@ -379,7 +389,7 @@
 
     hc = (m["hch"][...], m["hcl"][...])
     m["s0"][...] = leaf_rows(hc, diagonal(-w0, cap)) + m["low0"][...]
-    pl.semaphore_wait(ready, NEAR - 1 + ring - 1)
+    pl.semaphore_wait(ready.at[2], NEAR - 1 + ring - 1)
     send_leaf("s0", "r0", lambda q: q)
 
     def store_row(buf, i, row):
@@ -843,7 +853,7 @@
             pltpu.SemaphoreType.DMA((56,)),
             pltpu.SemaphoreType.DMA((56,)),
             pltpu.SemaphoreType.DMA((30,)),
-            pltpu.SemaphoreType.REGULAR,
+            pltpu.SemaphoreType.REGULAR((3,)),
         ]
         vspec = pl.BlockSpec(memory_space=pltpu.VMEM)
         whole = pl.pallas_call(

time: 79.1 us -> 78.8 us (level)
  no operation moved by 1% of the time
where the time goes in v7:
time: 78.8 us; the launch traced here: 78.7 us
  Pallas kernels  76.7 us (97%)
  local copies, waits for them, and re-layouts  1.3 us (2%)
    pallas_call x1, Pallas kernels, shards(): pl.pallas_call(functools.partial(kernel, (leaves, across, size, ups, coun...  76.7 us

profile of v7, /device:TPU:1, one launch (start us, length us, event | category | flops | bytes accessed | tf_op | source)
XLA Modules:
  0.0 78.7 jit_solution(14046616274519354268)
XLA Ops:
  0.6 76.7 %shard_map.309 = f32[32,128]{1,0:T(8,128)} custom-call(f32[8,128]{1,0:T(8,128)} %refs_0_.1, f32[8,128]{1,0:T(8,128)} %refs_1_.1, f32[8,128]{1,0:T(8,128)} %refs_2_.1, f32[8,128]{1,0:T(8,128)} %refs_3_.1, f32[128,128]{1,0:T(8,128)} %refs_4_.1, f32[128,128]{1,0:T(8,128)} %refs_5_.1, f32[128,128]{1,0:T(8,128)} %refs_6_.1, f32[128,128]{1,0:T(8,128)} %refs_7_.1, ...), custom_call_target="tpu_custom_call" | custom-call | tf_op jit(solution)/shard_map/pallas_call | solution.py:859
  77.4 1.3 %fusion = (f32[8,128]{1,0:T(8,128)}, f32[8,128]{1,0:T(8,128)}, f32[8,128]{1,0:T(8,128)}, f32[8,128]{1,0:T(8,128)}) fusion(f32[32,128]{1,0:T(8,128)} %shard_map.309), kind=kLoop, calls=%fused_computation | loop fusion | bytes 32768 | tf_op jit(solution)/shard_map/slice | solution.py:869

commit v8 on v7

--- a/solution.py
+++ b/solution.py
@@ -643,8 +643,6 @@
     inc = receive_up(1, sums_up(1))
     b2 = src[2][...] + inc[:, :LANES]
     send_up(2, b2, inc[:, LANES:])
-    m["yg"][near] = near_sum("yr")
-    spread_own("yg", NEAR, 1)
 
     local2 = mult(b2, blk[2][...])
     arrive("xg2")
@@ -664,6 +662,8 @@
     sr = sr + times(jnp.concatenate(passing, axis=1), halves(pulled), 0)
     m["sr"][near] = jnp.concatenate([sr[:, :RANK], sr[:, RANK:]], axis=0)
     spread_own("sr", NEAR, 1)
+    m["yg"][near] = near_sum("yr")
+    spread_own("yg", NEAR, 1)
     spread_own("c0", four, 1)
     solve_front(1, local1)
     tail_of(2, wv_of(2))

time: 78.8 us -> 79 us (level)
  no operation moved by 1% of the time
where the time goes in v8:
time: 79 us; the launch traced here: 78.8 us
  Pallas kernels  76.8 us (97%)
  local copies, waits for them, and re-layouts  1.3 us (2%)
    pallas_call x1, Pallas kernels, shards(): pl.pallas_call(functools.partial(kernel, (leaves, across, size, ups, coun...  76.8 us

profile of v8, /device:TPU:1, one launch (start us, length us, event | category | flops | bytes accessed | tf_op | source)
XLA Modules:
  0.0 78.8 jit_solution(923857403763944792)
XLA Ops:
  0.6 76.8 %shard_map.309 = f32[32,128]{1,0:T(8,128)} custom-call(f32[8,128]{1,0:T(8,128)} %refs_0_.1, f32[8,128]{1,0:T(8,128)} %refs_1_.1, f32[8,128]{1,0:T(8,128)} %refs_2_.1, f32[8,128]{1,0:T(8,128)} %refs_3_.1, f32[128,128]{1,0:T(8,128)} %refs_4_.1, f32[128,128]{1,0:T(8,128)} %refs_5_.1, f32[128,128]{1,0:T(8,128)} %refs_6_.1, f32[128,128]{1,0:T(8,128)} %refs_7_.1, ...), custom_call_target="tpu_custom_call" | custom-call | tf_op jit(solution)/shard_map/pallas_call | solution.py:859
  77.5 1.3 %fusion = (f32[8,128]{1,0:T(8,128)}, f32[8,128]{1,0:T(8,128)}, f32[8,128]{1,0:T(8,128)}, f32[8,128]{1,0:T(8,128)}) fusion(f32[32,128]{1,0:T(8,128)} %shard_map.309), kind=kLoop, calls=%fused_computation | loop fusion | bytes 32768 | tf_op jit(solution)/shard_map/slice | solution.py:869
